TPU v7x, 8 devices: a whole 2x2x1 slice. The times are simulated.
8 devices in a mesh: dp: 2 (over z, y), tp: 4 (over x, core).
Axes of the slice: x: 2, y: 2, z: 1, core: 2. Of those that a mesh axis runs over, the one named last changes fastest.
Arguments:
- x: bfloat16 [12, 256, 1536], P('dp', 'tp'), parts along dimension 0
- k_cache: bfloat16 [12, 3072, 4, 128], P('dp', None, 'tp'), parts along dimension 0
- v_cache: bfloat16 [12, 3072, 4, 128], P('dp', None, 'tp'), parts along dimension 0
- prefix_len: int32 [12], P('dp'), parts along dimension 0
- valid_len: int32 [12], P('dp'), parts along dimension 0
- g_attn: bfloat16 [1536], replicated
- w_q: bfloat16 [1536, 1536], P(None, 'tp')
- b_q: bfloat16 [1536], P('tp')
- w_k: bfloat16 [1536, 512], P(None, 'tp')
- b_k: bfloat16 [512], P('tp')
- w_v: bfloat16 [1536, 512], P(None, 'tp')
- b_v: bfloat16 [512], P('tp')
- w_o: bfloat16 [1536, 1536], P('tp')
- g_mlp: bfloat16 [1536], replicated
- w_gate: bfloat16 [1536, 8960], P(None, 'tp')
- w_up: bfloat16 [1536, 8960], P(None, 'tp')
- w_down: bfloat16 [8960, 1536], P('tp')
Outputs:
- output 1: bfloat16 [12, 256, 1536], P('dp', 'tp'), parts along dimension 0
- output 2: bfloat16 [12, 3072, 4, 128], P('dp', None, 'tp'), parts along dimension 0
- output 3: bfloat16 [12, 3072, 4, 128], P('dp', None, 'tp'), parts along dimension 0
There are 2 independent parts. A program takes and returns all parts, laid end to end along the dimension named above; an argument that names none is the same for every part.
All inputs are finite; a program needn't handle non-finite values.
Results may differ from a plain program's by a relative error of at most 0.0167596.
Values are sent between devices in bfloat16 or wider.
A program may use at most 1 GiB of HBM per device.

v0:
```python
import jax
import jax.numpy as jnp
import numpy as np
from jax import lax
from jax.experimental import pallas as pl
from jax.experimental.pallas import tpu as pltpu
from jax.sharding import PartitionSpec as P

ROPE_THETA = 1.0e6
NORM_EPS = 1.0e-6
LOG2E = 1.4426950408889634
MESH = pl.DeviceIdType.MESH
ANY = pl.BlockSpec(memory_space=pl.ANY)
VMEM = pl.BlockSpec(memory_space=pltpu.VMEM)
SMEM = pl.BlockSpec(memory_space=pltpu.SMEM)
DMA = pltpu.SemaphoreType.DMA
REQ = 6
ROWS = 64
WIDTH = 1536
HEAD = 128
FFN = 2240
FFN_PAD = 2304
FFN_TILE = 768
OUT_TILE = 768
GROUP = 3


def rms_norm(wide, gain):
    inv_rms = lax.rsqrt(jnp.mean(wide * wide, axis=-1, keepdims=True) + NORM_EPS)
    return (wide * inv_rms * gain).astype(jnp.bfloat16)


def partners():
    me = lax.axis_index("tp")
    chip, core = me // 2, me % 2
    return lax.axis_index("dp"), (me, chip * 2 + 1 - core, (1 - chip) * 2 + core, (1 - chip) * 2 + 1 - core)


def greet(devices):
    barrier = pltpu.get_barrier_semaphore()
    for device in devices:
        pl.semaphore_signal(barrier, inc=1, device_id=device, device_id_type=MESH)
    pl.semaphore_wait(barrier, len(devices))


def send(src, dst, send_sem, recv_sem, device):
    return pltpu.make_async_remote_copy(src_ref=src, dst_ref=dst, send_sem=send_sem, recv_sem=recv_sem, device_id=device, device_id_type=MESH)


def rope_tables():
    freq = ROPE_THETA ** (-(np.arange(HEAD // 2, dtype=np.float64) * 2.0) / HEAD)
    freq = np.concatenate([freq, freq])
    angles = np.arange(4 * ROWS, dtype=np.float64)[:, None] * freq
    return np.cos(angles).astype(np.float32), np.sin(angles).astype(np.float32), freq.astype(np.float32)[None]


def qkv_kernel(prefix_ref, x_ref, g_ref, bias_ref, cos_ref, sin_ref, freq_ref, wq_ref, wk_ref, wv_ref,
               q_ref, k_ref, v_ref, pair_ref,
               xbuf, wbuf, cbuf, sbuf, in_sem, w_sem, out_sem, sx, rx, sc, rc, sf, rf):
    dp, (me, core_peer, chip_peer, _) = partners()
    order = (me, core_peer, chip_peer, partners()[1][3])
    load_x = pltpu.make_async_copy(x_ref, xbuf.at[0], in_sem)
    load_x.start()
    loads = (
        pltpu.make_async_copy(wq_ref, wbuf.at[:, pl.ds(0, 384)], w_sem.at[0]),
        pltpu.make_async_copy(wk_ref, wbuf.at[:, pl.ds(384, 128)], w_sem.at[1]),
        pltpu.make_async_copy(wv_ref, wbuf.at[:, pl.ds(512, 128)], w_sem.at[2]),
    )
    for load in loads:
        load.start()
    greet([(dp, core_peer), (dp, chip_peer)])
    load_x.wait()

    def to_chip(r):
        return send(xbuf.at[0, r], xbuf.at[2, r], sx.at[r], rx.at[r], (dp, chip_peer))

    def to_core(r):
        return send(xbuf.at[0, r], xbuf.at[1, r], sc.at[r], rc.at[r], (dp, core_peer))

    def forward(r):
        return send(xbuf.at[2, r], xbuf.at[3, r], sf.at[r], rf.at[r], (dp, core_peer))

    def keep(r):
        return pltpu.make_async_copy(xbuf.at[2, r], pair_ref.at[r], out_sem.at[r])

    for r in range(REQ):
        to_chip(r).start()
    for r in range(REQ):
        to_core(r).start()
    for slot in range(4):
        rows = pl.ds(pl.multiple_of(order[slot] * ROWS, ROWS), ROWS)
        cbuf[slot * ROWS:(slot + 1) * ROWS, :] = cos_ref[rows, :]
        sbuf[slot * ROWS:(slot + 1) * ROWS, :] = sin_ref[rows, :]
    for load in loads:
        load.wait()
    lane = lax.broadcasted_iota(jnp.int32, (4 * ROWS, HEAD), 1)

    def project(r):
        wide = xbuf[:, r].reshape(4 * ROWS, WIDTH).astype(jnp.float32)
        normed = rms_norm(wide, g_ref[...].astype(jnp.float32))
        total = jnp.dot(normed, wbuf[...], preferred_element_type=jnp.float32)
        rounded = (total + bias_ref[...].astype(jnp.float32)).astype(jnp.bfloat16)
        angle = jnp.full((8, HEAD), prefix_ref[r], jnp.int32).astype(jnp.float32) * freq_ref[...]
        cos_p, sin_p = jnp.cos(angle)[:1], jnp.sin(angle)[:1]
        cos_t = cos_p * cbuf[...] - sin_p * sbuf[...]
        sin_t = sin_p * cbuf[...] + cos_p * sbuf[...]
        sin_t = jnp.where(lane < HEAD // 2, -sin_t, sin_t)
        for head in range(4):
            part = rounded[:, head * HEAD:(head + 1) * HEAD].astype(jnp.float32)
            turned = (part * cos_t + pltpu.roll(part, HEAD // 2, 1) * sin_t).astype(jnp.bfloat16)
            for slot in range(4):
                rows = pl.ds(pl.multiple_of(order[slot] * ROWS, ROWS), ROWS)
                piece = turned[slot * ROWS:(slot + 1) * ROWS]
                if head < 3:
                    q_ref[r, head, rows, :] = piece
                else:
                    k_ref[r, rows, :] = piece
        for slot in range(4):
            rows = pl.ds(pl.multiple_of(order[slot] * ROWS, ROWS), ROWS)
            v_ref[r, rows, :] = rounded[slot * ROWS:(slot + 1) * ROWS, 4 * HEAD:]

    @pl.loop(0, REQ + 1)
    def _(r):
        @pl.when(r < REQ)
        def _():
            to_chip(r).wait_recv()
            forward(r).start()
            keep(r).start()

        @pl.when(r > 0)
        def _():
            to_core(r - 1).wait_recv()
            forward(r - 1).wait_recv()
            project(r - 1)

    @pl.loop(0, REQ)
    def _(r):
        to_chip(r).wait_send()
        to_core(r).wait_send()
        forward(r).wait_send()
        keep(r).wait()


def project_rows(prefix, x_rows, g_attn, bias, w_q, w_k, w_v):
    cos_i, sin_i, freq = rope_tables()
    return pl.pallas_call(
        qkv_kernel,
        in_specs=[SMEM, ANY, VMEM, VMEM, VMEM, VMEM, VMEM, ANY, ANY, ANY],
        out_specs=[VMEM, VMEM, VMEM, ANY],
        out_shape=[
            jax.ShapeDtypeStruct((REQ, 3, 4 * ROWS, HEAD), jnp.bfloat16),
            jax.ShapeDtypeStruct((REQ, 4 * ROWS, HEAD), jnp.bfloat16),
            jax.ShapeDtypeStruct((REQ, 4 * ROWS, HEAD), jnp.bfloat16),
            jax.ShapeDtypeStruct((REQ, ROWS, WIDTH), jnp.bfloat16),
        ],
        scratch_shapes=[
            pltpu.VMEM((4, REQ, ROWS, WIDTH), jnp.bfloat16),
            pltpu.VMEM((WIDTH, 640), jnp.bfloat16),
            pltpu.VMEM((4 * ROWS, HEAD), jnp.float32),
            pltpu.VMEM((4 * ROWS, HEAD), jnp.float32),
            DMA, DMA((3,)), DMA((REQ,)),
            DMA((REQ,)), DMA((REQ,)), DMA((REQ,)), DMA((REQ,)), DMA((REQ,)), DMA((REQ,)),
        ],
        compiler_params=pltpu.CompilerParams(collective_id=0, has_side_effects=True),
        name="exchange_qkv",
    )(prefix, x_rows, g_attn[None], bias, cos_i, sin_i, freq, w_q, w_k, w_v)


BLOCK_KV = 512
WINDOW = 272


def merge_rows(old_ref, fresh_ref, out_ref, start, count):
    slots = old_ref.shape[1]
    out_ref[0] = old_ref[0]
    base = pl.multiple_of(jnp.minimum((start // 16) * 16, slots - WINDOW), 16)
    shift = start - base
    fresh = fresh_ref[0].astype(jnp.float32)
    padded = jnp.concatenate([fresh, jnp.zeros((WINDOW - fresh.shape[0], fresh.shape[1]), jnp.float32)], axis=0)
    rolled = pltpu.roll(padded, shift, 0)
    idx = lax.broadcasted_iota(jnp.int32, rolled.shape, 0) - shift
    window = out_ref[0, pl.ds(base, WINDOW), :].astype(jnp.float32)
    merged = jnp.where((idx >= 0) & (idx < count), rolled, window)
    out_ref[0, pl.ds(base, WINDOW), :] = merged.astype(jnp.bfloat16)


def attn_kernel(prefix_ref, valid_ref, q_ref, kn_ref, vn_ref, k_ref, v_ref, o_ref, ko_ref, vo_ref, acc_ref, m_ref, l_ref):
    req = pl.program_id(0)
    start = prefix_ref[req]
    count = valid_ref[req]
    merge_rows(k_ref, kn_ref, ko_ref, start, count)
    merge_rows(v_ref, vn_ref, vo_ref, start, count)
    heads, rows, dim = q_ref.shape[1:]
    factor = (dim ** -0.5) * LOG2E
    acc_ref[...] = jnp.zeros_like(acc_ref)
    l_ref[...] = jnp.zeros_like(l_ref)
    m_ref[...] = jnp.full_like(m_ref, -1.0e30)
    n_full = start // BLOCK_KV
    n_all = (start + count + BLOCK_KV - 1) // BLOCK_KV

    def step(blk, masked):
        off = pl.multiple_of(blk * BLOCK_KV, BLOCK_KV)
        keys = ko_ref[0, pl.ds(off, BLOCK_KV), :]
        vals = vo_ref[0, pl.ds(off, BLOCK_KV), :]
        if masked:
            row = lax.broadcasted_iota(jnp.int32, (rows, BLOCK_KV), 0)
            col = lax.broadcasted_iota(jnp.int32, (rows, BLOCK_KV), 1)
            visible = col + off <= start + jnp.minimum(row, count - 1)
        for h in range(heads):
            s = lax.dot_general(q_ref[0, h], keys, (((1,), (1,)), ((), ())), preferred_element_type=jnp.float32)
            if masked:
                s = jnp.where(visible, s, -1.0e30)
            m_old = m_ref[h]
            m_new = jnp.maximum(m_old, jnp.max(s, axis=1, keepdims=True) * factor)
            alpha = jnp.exp2(m_old - m_new)
            p = jnp.exp2(s * factor - m_new[:, :1])
            part = p[:, :128]
            for j in range(1, BLOCK_KV // 128):
                part = part + p[:, j * 128:(j + 1) * 128]
            l_ref[h] = l_ref[h] * alpha + part
            m_ref[h] = m_new
            acc_ref[h] = acc_ref[h] * alpha + jnp.dot(p.astype(jnp.bfloat16), vals, preferred_element_type=jnp.float32)

    @pl.loop(0, n_full)
    def _(blk):
        step(blk, False)

    @pl.loop(n_full, n_all)
    def _(blk):
        step(blk, True)

    for h in range(heads):
        total = jnp.sum(l_ref[h], axis=1, keepdims=True)
        o_ref[0, :, h * dim:(h + 1) * dim] = (acc_ref[h] / total).astype(jnp.bfloat16)


def attention(prefix, valid, q, kn, vn, k_cache, v_cache):
    n_req, heads, rows, dim = q.shape
    slots = k_cache.shape[1]
    new_spec = pl.BlockSpec((1, rows, dim), lambda r, *_: (r, 0, 0))
    cache_spec = pl.BlockSpec((1, slots, dim), lambda r, *_: (r, 0, 0))
    return pl.pallas_call(
        attn_kernel,
        grid_spec=pltpu.PrefetchScalarGridSpec(
            num_scalar_prefetch=2,
            grid=(n_req,),
            in_specs=[pl.BlockSpec((1, heads, rows, dim), lambda r, *_: (r, 0, 0, 0)), new_spec, new_spec, cache_spec, cache_spec],
            out_specs=[pl.BlockSpec((1, rows, heads * dim), lambda r, *_: (r, 0, 0)), cache_spec, cache_spec],
            scratch_shapes=[pltpu.VMEM((heads, rows, dim), jnp.float32)] * 3,
        ),
        out_shape=[
            jax.ShapeDtypeStruct((n_req, rows, heads * dim), jnp.bfloat16),
            jax.ShapeDtypeStruct(k_cache.shape, jnp.bfloat16),
            jax.ShapeDtypeStruct(v_cache.shape, jnp.bfloat16),
        ],
        compiler_params=pltpu.CompilerParams(dimension_semantics=("arbitrary",)),
        name="attention",
    )(prefix, valid, q, kn, vn, k_cache, v_cache)


def mlp_kernel(o_ref, x_ref, pair_ref, g_ref, wo_ref, wx_ref, wg_ref, wu_ref, wd_ref, out_ref,
               obuf, xin, wo, wg, wu, wd, hbuf, ubuf, psend, precv, pown, xsend, xrecv, x1buf,
               w_sem, wl_sem, in_sem, so, ro, lo, swy, rwy, swc, rwc, sh, rh, sp, rp, ss, rs):
    dp, peers = partners()
    me, core_peer, chip_peer, far_peer = peers
    other_dp = 1 - dp
    half = 192

    def cols(who):
        return pl.ds(pl.multiple_of(who * 384, 384), 384)

    def share(slot, g, s):
        block = peers[s] if slot == 0 else peers[s ^ 2]
        src = o_ref.at[pl.ds(GROUP * g, GROUP), block]
        dst = obuf.at[slot, pl.ds(GROUP * g, GROUP), :, cols(me)]
        if s == 0:
            return pltpu.make_async_copy(src, dst, lo.at[slot, g])
        return send(src, dst, so.at[slot, g, s - 1], ro.at[slot, g, s - 1], (dp, peers[s]))

    def wo_rows(block, part):
        return pl.ds(pl.multiple_of(block * 384 + part * half, half), half)

    own_rows = pl.ds(pl.multiple_of(me * 384, 384), 384)
    near = wo_rows(chip_peer, dp)
    across = wo_rows(chip_peer, other_dp)
    wo_local = (
        pltpu.make_async_copy(wo_ref, wo.at[own_rows], wl_sem.at[0]),
        pltpu.make_async_copy(wx_ref, wo.at[near], wl_sem.at[1]),
    )
    wo_dp = send(wx_ref, wo.at[near], swy, rwy, (other_dp, me))
    wo_core = (
        send(wo_ref, wo.at[own_rows], swc.at[0], rwc.at[0], (dp, core_peer)),
        send(wx_ref, wo.at[near], swc.at[1], rwc.at[1], (dp, core_peer)),
        send(wo.at[across], wo.at[across], swc.at[2], rwc.at[2], (dp, core_peer)),
    )
    weights = (
        pltpu.make_async_copy(wg_ref, wg.at[pl.ds(0, FFN)], w_sem.at[0]),
        pltpu.make_async_copy(wu_ref, wu.at[pl.ds(0, FFN)], w_sem.at[1]),
        pltpu.make_async_copy(wd_ref, wd.at[pl.ds(0, FFN)], w_sem.at[2]),
    )
    x_loads = (
        pltpu.make_async_copy(x_ref, xin.at[0], in_sem.at[0]),
        pltpu.make_async_copy(pair_ref, xin.at[1], in_sem.at[1]),
    )
    order = ((1, 0), (1, 1), (0, 0), (0, 1))

    greet([(dp, core_peer), (dp, chip_peer), (dp, far_peer), (other_dp, me)])
    wo_dp.start()
    for slot, g in order:
        for s in (2, 3, 1):
            share(slot, g, s).start()
    for copy in wo_core[:2] + wo_local:
        copy.start()
    for slot, g in order:
        share(slot, g, 0).start()
    for copy in x_loads + weights:
        copy.start()
    pad = jnp.zeros((FFN_PAD - FFN, WIDTH), jnp.bfloat16)
    for buf in (wg, wu, wd):
        buf[FFN:, :] = pad

    gain = g_ref[...].astype(jnp.float32)

    def give_h(k):
        return send(hbuf.at[k, 0], hbuf.at[k, 1], sh.at[k], rh.at[k], (dp, core_peer))

    def give_p(k):
        return send(psend.at[k], precv.at[k], sp.at[k], rp.at[k], (dp, core_peer))

    def give_s(g):
        return send(xsend.at[g], xrecv.at[g], ss.at[g], rs.at[g], (dp, chip_peer))

    def attn_out(k):
        slot, g = order[k]
        for s in (2, 3, 1):
            share(slot, g, s).wait_recv()
        share(slot, g, 0).wait()
        reqs = slice(GROUP * g, GROUP * (g + 1))
        heads = obuf[slot, reqs].reshape(GROUP * ROWS, WIDTH)
        attn = jnp.dot(heads, wo[...], preferred_element_type=jnp.float32).astype(jnp.bfloat16)
        base = xin[slot, reqs].reshape(GROUP * ROWS, WIDTH)
        mid = (base.astype(jnp.float32) + attn.astype(jnp.float32)).astype(jnp.bfloat16)
        if slot == 0:
            x1buf[g] = mid
        hbuf[k, 0] = rms_norm(mid.astype(jnp.float32), gain)
        give_h(k).start()

    def mlp(k):
        give_h(k).wait_recv()
        hidden = hbuf.at[k].reshape(2 * GROUP * ROWS, WIDTH)

        @pl.loop(0, FFN_PAD // FFN_TILE)
        def _(f):
            at = pl.ds(pl.multiple_of(f * FFN_TILE, FFN_TILE), FFN_TILE)
            nt = (((1,), (1,)), ((), ()))
            gate = lax.dot_general(hidden[...], wg[at, :], nt, preferred_element_type=jnp.float32)
            up = lax.dot_general(hidden[...], wu[at, :], nt, preferred_element_type=jnp.float32)
            ubuf[:, at] = (jax.nn.silu(gate) * up).astype(jnp.bfloat16)

        @pl.loop(0, WIDTH // OUT_TILE)
        def _(n):
            at = pl.ds(pl.multiple_of(n * OUT_TILE, OUT_TILE), OUT_TILE)
            down = jnp.dot(ubuf[...], wd[:, at], preferred_element_type=jnp.float32)
            pown[k, :, at] = down[:GROUP * ROWS]
            psend[k, :, at] = down[GROUP * ROWS:].astype(jnp.bfloat16)

        give_p(k).start()

    def combine(k):
        slot, g = order[k]
        give_p(k).wait_recv()
        total = pown[k] + precv[k].astype(jnp.float32)
        if slot == 1:
            xsend[g] = total.astype(jnp.bfloat16)
            give_s(g).start()
        else:
            give_s(g).wait_recv()
            down = (total + xrecv[g].astype(jnp.float32)).astype(jnp.bfloat16)
            out = (x1buf[g].astype(jnp.float32) + down.astype(jnp.float32)).astype(jnp.bfloat16)
            out_ref[GROUP * g:GROUP * (g + 1)] = out.reshape(GROUP, ROWS, WIDTH)

    wo_dp.wait_recv()
    wo_core[2].start()
    for copy in wo_local + x_loads:
        copy.wait()
    for copy in wo_core:
        copy.wait_recv()
    attn_out(0)
    for copy in weights:
        copy.wait()
    mlp(0)
    attn_out(1)
    attn_out(2)
    combine(0)
    mlp(1)
    attn_out(3)
    combine(1)
    mlp(2)
    mlp(3)
    combine(2)
    combine(3)
    wo_dp.wait_send()
    for copy in wo_core:
        copy.wait_send()
    for k, (slot, g) in enumerate(order):
        for s in (2, 3, 1):
            share(slot, g, s).wait_send()
        give_h(k).wait_send()
        give_p(k).wait_send()
    for g in range(2):
        give_s(g).wait_send()


def finish_layer(o, x_rows, x_pair, g_mlp, w_o, w_x, w_gate_t, w_up_t, w_down):
    block = GROUP * ROWS
    return pl.pallas_call(
        mlp_kernel,
        in_specs=[ANY, ANY, ANY, VMEM, ANY, ANY, ANY, ANY, ANY],
        out_specs=VMEM,
        out_shape=jax.ShapeDtypeStruct((REQ, ROWS, WIDTH), jnp.bfloat16),
        scratch_shapes=[
            pltpu.VMEM((2, REQ, ROWS, WIDTH), jnp.bfloat16),
            pltpu.VMEM((2, REQ, ROWS, WIDTH), jnp.bfloat16),
            pltpu.VMEM((WIDTH, WIDTH), jnp.bfloat16),
            pltpu.VMEM((FFN_PAD, WIDTH), jnp.bfloat16),
            pltpu.VMEM((FFN_PAD, WIDTH), jnp.bfloat16),
            pltpu.VMEM((FFN_PAD, WIDTH), jnp.bfloat16),
            pltpu.VMEM((4, 2, block, WIDTH), jnp.bfloat16),
            pltpu.VMEM((2 * block, FFN_PAD), jnp.bfloat16),
            pltpu.VMEM((4, block, WIDTH), jnp.bfloat16),
            pltpu.VMEM((4, block, WIDTH), jnp.bfloat16),
            pltpu.VMEM((4, block, WIDTH), jnp.float32),
            pltpu.VMEM((2, block, WIDTH), jnp.bfloat16),
            pltpu.VMEM((2, block, WIDTH), jnp.bfloat16),
            pltpu.VMEM((2, block, WIDTH), jnp.bfloat16),
            DMA((3,)), DMA((2,)), DMA((2,)),
            DMA((2, 2, 3)), DMA((2, 2, 3)), DMA((2, 2)),
            DMA, DMA, DMA((3,)), DMA((3,)),
            DMA((4,)), DMA((4,)), DMA((4,)), DMA((4,)), DMA((2,)), DMA((2,)),
        ],
        compiler_params=pltpu.CompilerParams(collective_id=1, has_side_effects=True, vmem_limit_bytes=62 * 1024 * 1024),
        name="finish_layer",
    )(o, x_rows, x_pair, g_mlp[None], w_o, w_x, w_gate_t, w_up_t, w_down)


def solution(mesh):
    row_spec = P("dp", "tp", None)
    cache_spec = P("dp", None, "tp", None)
    req_spec = P("dp")
    rep_spec = P(None)
    col_spec = P(None, "tp")
    bias_spec = P("tp")
    down_spec = P("tp", None)

    def layer(x_rows, k_cache, v_cache, prefix, valid, g_attn, w_q, b_q, w_k, b_k, w_v, b_v, w_o, g_mlp, w_gate, w_up, w_down):
        cache_shape = (REQ, k_cache.shape[1], HEAD)
        bias = jnp.concatenate([b_q, b_k, b_v])[None]
        q, k_new, v_new, x_pair = project_rows(prefix, x_rows, g_attn, bias, w_q, w_k, w_v)
        w_half = lax.dynamic_slice_in_dim(w_o, lax.axis_index("dp") * 192, 192, axis=0)
        w_half, q = lax.optimization_barrier((w_half, q))
        w_x = lax.ppermute(w_half, "tp", [(0, 2), (1, 3), (2, 0), (3, 1)])
        o, k_out, v_out = attention(prefix, valid, q, k_new, v_new, k_cache.reshape(cache_shape), v_cache.reshape(cache_shape))
        x_out = finish_layer(o.reshape(REQ, 4, ROWS, 3 * HEAD), x_rows, x_pair, g_mlp, w_o, w_x, w_gate.T, w_up.T, w_down)
        return x_out, k_out.reshape(k_cache.shape), v_out.reshape(v_cache.shape)

    in_specs = (row_spec, cache_spec, cache_spec, req_spec, req_spec, rep_spec, col_spec, bias_spec, col_spec, bias_spec, col_spec, bias_spec, down_spec, rep_spec, col_spec, col_spec, down_spec)
    return jax.shard_map(layer, mesh=mesh, in_specs=in_specs, out_specs=(row_spec, cache_spec, cache_spec), check_vma=False)
```

profile of v0, /device:TPU:0, one launch (start us, length us, event | category | flops | bytes accessed | tf_op | source)
XLA Modules:
  0.0 151.3 jit_solution(9261710980341390911)
XLA Ops:
  0.6 1.3 broadcast_in_dim.9.g_ref
  1.9 0.7 pad_maximum_fusion
  2.6 0.6 broadcast_in_dim.10.bias_ref
  3.2 1.1 constant_dynamic-slice_fusion
  4.3 0.0 copy-start.1
  4.3 35.8 %exchange_qkv.1 = (bf16[6,3,256,128]{3,2,1,0:T(8,128)(2,1)}, bf16[6,256,128]{2,1,0:T(8,128)(2,1)}, bf16[6,256,128]{2,1,0:T(8,128)(2,1)}, bf16[6,64,1536]{2,1,0:T(8,128)(2,1)}) custom-call(s32[6]{0:T(128)} %prefix_ref.3, bf16[6,64,1536]{2,1,0:T(8,128)(2,1)} %x_ref.3, bf16[1,1536]{1,0:T(2,128)(2,1)} %broadcast_in_dim.9.g_ref, ...), custom_call_target="tpu_custom_call" | custom-call | tf_op jit(solution)/shard_map/exchange_qkv/pallas_call | solution.py:146
  40.1 0.0 collective-permute-start
  40.1 0.0 copy-done.1
  40.2 0.6 broadcast_in_dim.11.g_ref
  40.7 39.6 %attention.1 = (bf16[6,256,384]{2,1,0:T(8,128)(2,1)}, bf16[6,3072,128]{2,1,0:T(8,128)(2,1)}, bf16[6,3072,128]{2,1,0:T(8,128)(2,1)}) custom-call(s32[6]{0:T(128)} %prefix_ref.3, s32[6]{0:T(128)} %valid_ref.1, bf16[6,3,256,128]{3,2,1,0:T(8,128)(2,1)} %get-tuple-element.13.q_ref, bf16[6,256,128]{2,1,0:T(8,128)(2,1)} %get-tuple-element.14.kn_ref, ...), custom_call_target="tpu_custom_call" | custom-call | tf_op jit(solution)/shard_map/attention/pallas_call | solution.py:242
  80.4 0.0 collective-permute-done.wx_ref
  80.4 0.0 copy-start
  80.4 0.8 copy-done
  81.2 67.7 %finish_layer.1 = bf16[6,64,1536]{2,1,0:T(8,128)(2,1)} custom-call(bf16[6,4,64,384]{3,2,1,0:T(8,128)(2,1)} %bitcast.15, bf16[6,64,1536]{2,1,0:T(8,128)(2,1)} %x_ref.3, bf16[6,64,1536]{2,1,0:T(8,128)(2,1)} %get-tuple-element.17.pair_ref, bf16[1,1536]{1,0:T(2,128)(2,1)} %broadcast_in_dim.11.g_ref, bf16[384,1536]{1,0:T(8,128)(2,1)} %wo_ref.1, ...), custom_call_target="tpu_custom_call" | custom-call | tf_op jit(solution)/shard_map/finish_layer/pallas_call | solution.py:416
  148.9 2.4 %copy.26 = bf16[6,64,1536]{2,1,0:T(8,128)(2,1)} copy(bf16[6,64,1536]{2,1,0:T(8,128)(2,1)} %finish_layer.1) | data formatting | bytes 2359296
Async XLA Ops:
  4.3 35.8 %copy-start.1 = (bf16[1536]{0:T(1024)(128)(2,1)S(1)}, bf16[1536]{0:T(1024)(128)(2,1)}, u32[]{:S(2)}) copy-start(bf16[1536]{0:T(1024)(128)(2,1)} %param.33) | copy-start | bytes 9220
  40.1 40.3 %collective-permute-start = (bf16[192,1536]{1,0:T(8,128)(2,1)S(1)}, bf16[192,1536]{1,0:T(8,128)(2,1)S(1)}, u32[]{:S(2)}, u32[]{:S(2)}) collective-permute-start(bf16[192,1536]{1,0:T(8,128)(2,1)S(1)} %constant_dynamic-slice_fusion), channel_id=1, source_target_pairs={{0,2},{1,3},{2,0},{3,1},{4,6},{5,7},{6,4},{7,5}} | collective-permute-start | bytes 1769480 | tf_op jit(solution)/shard_map/ppermute | solution.py:461
  80.4 0.8 copy-start
where the time goes:
time: 152 us; the launch traced here: 151 us
  Pallas kernels  143 us (94%)
  local copies, waits for them, and re-layouts  6.75 us (4%)
    pallas_call x1, Pallas kernels, finish_layer(): pl.pallas_call(mlp_kernel, in_specs=[ANY, ANY, ANY, VMEM, ANY, ANY, ANY,...  67.7 us
    pallas_call x1, Pallas kernels, attention(): pl.pallas_call(attn_kernel, grid_spec=pltpu.PrefetchScalarGridSpec(num_sc...  39.6 us
    pallas_call x1, Pallas kernels, project_rows(): pl.pallas_call(qkv_kernel, in_specs=[SMEM, ANY, VMEM, VMEM, VMEM, VMEM, V...  35.8 us
    unnamed x5, local copies, waits for them, and re-layouts  3.2 us
  transfers between devices with their start and end apart: 1, of which 0 were waited for; matrix products, arithmetic and copies ran while one was open for 0% of the time, Pallas kernels for 26%

commit v1 on v0

v1 whole, which is shorter than its diff:
```python
import functools

import jax
import jax.numpy as jnp
import numpy as np
from jax import lax
from jax.experimental import pallas as pl
from jax.experimental.pallas import tpu as pltpu
from jax.sharding import PartitionSpec as P

ROPE_THETA = 1.0e6
NORM_EPS = 1.0e-6
LOG2E = 1.4426950408889634
MESH = pl.DeviceIdType.MESH
ANY = pl.BlockSpec(memory_space=pl.ANY)
VMEM = pl.BlockSpec(memory_space=pltpu.VMEM)
SMEM = pl.BlockSpec(memory_space=pltpu.SMEM)
DMA = pltpu.SemaphoreType.DMA
REQ = 6
HALF_REQ = 3
ROWS = 64
WIDTH = 1536
HEAD = 128
FFN = 2240
FFN_PAD = 2304
FFN_TILE = 768
OUT_TILE = 768
GROUP = 3
WO_FIRST = 64
WO_REST = 128


def rms_norm(wide, gain):
    inv_rms = lax.rsqrt(jnp.mean(wide * wide, axis=-1, keepdims=True) + NORM_EPS)
    return (wide * inv_rms * gain).astype(jnp.bfloat16)


def partners():
    me = lax.axis_index("tp")
    chip, core = me // 2, me % 2
    return lax.axis_index("dp"), (me, chip * 2 + 1 - core, (1 - chip) * 2 + core, (1 - chip) * 2 + 1 - core)


def greet(devices):
    barrier = pltpu.get_barrier_semaphore()
    for device in devices:
        pl.semaphore_signal(barrier, inc=1, device_id=device, device_id_type=MESH)
    pl.semaphore_wait(barrier, len(devices))


def send(src, dst, send_sem, recv_sem, device):
    return pltpu.make_async_remote_copy(src_ref=src, dst_ref=dst, send_sem=send_sem, recv_sem=recv_sem, device_id=device, device_id_type=MESH)


def rope_tables():
    freq = ROPE_THETA ** (-(np.arange(HEAD // 2, dtype=np.float64) * 2.0) / HEAD)
    freq = np.concatenate([freq, freq])
    angles = np.arange(4 * ROWS, dtype=np.float64)[:, None] * freq
    return np.cos(angles).astype(np.float32), np.sin(angles).astype(np.float32), freq.astype(np.float32)[None]


def load_weights(wq_ref, wk_ref, wv_ref, wbuf, w_sem):
    return (
        pltpu.make_async_copy(wq_ref, wbuf.at[:, pl.ds(0, 384)], w_sem.at[0]),
        pltpu.make_async_copy(wk_ref, wbuf.at[:, pl.ds(384, 128)], w_sem.at[1]),
        pltpu.make_async_copy(wv_ref, wbuf.at[:, pl.ds(512, 128)], w_sem.at[2]),
    )


def project(x, position, chip, g_ref, biases, tables, wbuf, q_ref, k_ref, v_ref, r):
    cos_ref, sin_ref, freq_ref = tables
    rows = pl.ds(pl.multiple_of(chip * 2 * ROWS, 2 * ROWS), 2 * ROWS)
    normed = rms_norm(x.astype(jnp.float32), g_ref[...].astype(jnp.float32).reshape(1, WIDTH))
    total = jnp.dot(normed, wbuf[...], preferred_element_type=jnp.float32)
    angle = jnp.full((8, HEAD), position, jnp.int32).astype(jnp.float32) * freq_ref[...]
    cos_p, sin_p = jnp.cos(angle)[:1], jnp.sin(angle)[:1]
    cos_i, sin_i = cos_ref[rows, :], sin_ref[rows, :]
    cos_t = cos_p * cos_i - sin_p * sin_i
    sin_t = sin_p * cos_i + cos_p * sin_i
    lane = lax.broadcasted_iota(jnp.int32, sin_t.shape, 1)
    sin_t = jnp.where(lane < HEAD // 2, -sin_t, sin_t)
    bias = jnp.concatenate([b[...].astype(jnp.float32).reshape(1, b.shape[0]) for b in biases], axis=1)
    rounded = (total + bias).astype(jnp.bfloat16)
    for head in range(4):
        part = rounded[:, head * HEAD:(head + 1) * HEAD].astype(jnp.float32)
        turned = (part * cos_t + pltpu.roll(part, HEAD // 2, 1) * sin_t).astype(jnp.bfloat16)
        if head < 3:
            q_ref[r, head] = turned
        else:
            k_ref[r] = turned
    v_ref[r] = rounded[:, 4 * HEAD:]


def first_kernel(prefix_ref, x_ref, g_ref, bq_ref, bk_ref, bv_ref, cos_ref, sin_ref, freq_ref, wq_ref, wk_ref, wv_ref, wo_ref,
                 qa_ref, ka_ref, va_ref, qb_ref, kb_ref, vb_ref, pair_ref, first_ref, rest_ref,
                 own, other, wbuf, wpart, in_sem, w_sem, out_sem, wo_sem, sx, rx, sc, rc, sf, rf):
    dp, (me, core_peer, chip_peer, _) = partners()
    chip, core = me // 2, me % 2
    load_x = pltpu.make_async_copy(x_ref, own.at[core], in_sem)
    load_x.start()
    loads = load_weights(wq_ref, wk_ref, wv_ref, wbuf, w_sem)
    for load in loads:
        load.start()
    load_wo = pltpu.make_async_copy(wo_ref.at[pl.ds(pl.multiple_of(dp * 192, 192), 192)], wpart, wo_sem.at[0])
    load_wo.start()
    greet([(dp, core_peer), (dp, chip_peer)])
    load_x.wait()

    def to_chip(r):
        return send(own.at[core, r], other.at[core, r], sx.at[r], rx.at[r], (dp, chip_peer))

    def to_core(r):
        return send(own.at[core, r], own.at[core, r], sc.at[r], rc.at[r], (dp, core_peer))

    def forward(r):
        return send(other.at[core, r], other.at[core, r], sf.at[r], rf.at[r], (dp, core_peer))

    def keep(r):
        return pltpu.make_async_copy(other.at[core, r], pair_ref.at[r], out_sem.at[r])

    for r in range(HALF_REQ):
        to_chip(r).start()
    for r in range(REQ):
        to_core(r).start()
    load_wo.wait()
    give_wo = (
        pltpu.make_async_copy(wpart.at[pl.ds(0, WO_FIRST)], first_ref, wo_sem.at[1]),
        pltpu.make_async_copy(wpart.at[pl.ds(WO_FIRST, WO_REST)], rest_ref, wo_sem.at[2]),
    )
    for copy in give_wo:
        copy.start()
    for load in loads:
        load.wait()
    biases = (bq_ref, bk_ref, bv_ref)
    tables = (cos_ref, sin_ref, freq_ref)

    @pl.loop(0, REQ)
    def _(r):
        to_core(r).wait_recv()
        project(own[:, r].reshape(2 * ROWS, WIDTH), prefix_ref[r], chip, g_ref, biases, tables, wbuf, qa_ref, ka_ref, va_ref, r)

    @pl.loop(0, HALF_REQ + 1)
    def _(r):
        @pl.when(r < HALF_REQ)
        def _():
            to_chip(r).wait_recv()
            forward(r).start()
            keep(r).start()

        @pl.when(r > 0)
        def _():
            forward(r - 1).wait_recv()
            project(other[:, r - 1].reshape(2 * ROWS, WIDTH), prefix_ref[r - 1], 1 - chip, g_ref, biases, tables, wbuf, qb_ref, kb_ref, vb_ref, r - 1)

    for copy in give_wo:
        copy.wait()

    @pl.loop(0, REQ)
    def _(r):
        to_core(r).wait_send()

    @pl.loop(0, HALF_REQ)
    def _(r):
        to_chip(r).wait_send()
        forward(r).wait_send()
        keep(r).wait()


def second_kernel(prefix_ref, pair_ref, g_ref, bq_ref, bk_ref, bv_ref, cos_ref, sin_ref, freq_ref, wq_ref, wk_ref, wv_ref,
                  qb_ref, kb_ref, vb_ref, other, wbuf, in_sem, w_sem, sf, rf):
    dp, (me, core_peer, _, _) = partners()
    chip, core = me // 2, me % 2

    def load(r):
        return pltpu.make_async_copy(pair_ref.at[r], other.at[core, r], in_sem.at[r])

    def forward(r):
        return send(other.at[core, r], other.at[core, r], sf.at[r], rf.at[r], (dp, core_peer))

    for r in range(HALF_REQ):
        load(r).start()
    loads = load_weights(wq_ref, wk_ref, wv_ref, wbuf, w_sem)
    for copy in loads:
        copy.start()
    greet([(dp, core_peer)])
    for r in range(HALF_REQ):
        load(r).wait()
        forward(r).start()
    for copy in loads:
        copy.wait()

    @pl.loop(0, HALF_REQ)
    def _(r):
        forward(r).wait_recv()
        project(other[:, r].reshape(2 * ROWS, WIDTH), prefix_ref[HALF_REQ + r], 1 - chip, g_ref, (bq_ref, bk_ref, bv_ref), (cos_ref, sin_ref, freq_ref), wbuf, qb_ref, kb_ref, vb_ref, r)

    @pl.loop(0, HALF_REQ)
    def _(r):
        forward(r).wait_send()


def qkv_shapes(n_req):
    return [
        jax.ShapeDtypeStruct((n_req, 3, 2 * ROWS, HEAD), jnp.bfloat16),
        jax.ShapeDtypeStruct((n_req, 2 * ROWS, HEAD), jnp.bfloat16),
        jax.ShapeDtypeStruct((n_req, 2 * ROWS, HEAD), jnp.bfloat16),
    ]


def project_first(prefix, x_rows, shared, weights, w_o):
    return pl.pallas_call(
        first_kernel,
        in_specs=[SMEM, ANY] + [VMEM] * 7 + [ANY] * 4,
        out_specs=[VMEM] * 6 + [ANY] * 3,
        out_shape=qkv_shapes(REQ) + qkv_shapes(HALF_REQ) + [
            jax.ShapeDtypeStruct((HALF_REQ, ROWS, WIDTH), jnp.bfloat16),
            jax.ShapeDtypeStruct((WO_FIRST, WIDTH), jnp.bfloat16),
            jax.ShapeDtypeStruct((WO_REST, WIDTH), jnp.bfloat16),
        ],
        scratch_shapes=[
            pltpu.VMEM((2, REQ, ROWS, WIDTH), jnp.bfloat16),
            pltpu.VMEM((2, HALF_REQ, ROWS, WIDTH), jnp.bfloat16),
            pltpu.VMEM((WIDTH, 640), jnp.bfloat16),
            pltpu.VMEM((192, WIDTH), jnp.bfloat16),
            DMA, DMA((3,)), DMA((HALF_REQ,)), DMA((3,)),
            DMA((HALF_REQ,)), DMA((HALF_REQ,)), DMA((REQ,)), DMA((REQ,)), DMA((HALF_REQ,)), DMA((HALF_REQ,)),
        ],
        compiler_params=pltpu.CompilerParams(collective_id=0, has_side_effects=True),
        cost_estimate=pl.CostEstimate(flops=2 * 10 ** 9, bytes_accessed=60 * 10 ** 6, transcendentals=0),
        name="project_first",
    )(prefix, x_rows, *shared, *weights, w_o)


def project_second(prefix, pair, shared, weights):
    return pl.pallas_call(
        second_kernel,
        in_specs=[SMEM, ANY] + [VMEM] * 7 + [ANY] * 3,
        out_specs=[VMEM] * 3,
        out_shape=qkv_shapes(HALF_REQ),
        scratch_shapes=[
            pltpu.VMEM((2, HALF_REQ, ROWS, WIDTH), jnp.bfloat16),
            pltpu.VMEM((WIDTH, 640), jnp.bfloat16),
            DMA((HALF_REQ,)), DMA((3,)), DMA((HALF_REQ,)), DMA((HALF_REQ,)),
        ],
        compiler_params=pltpu.CompilerParams(collective_id=2, has_side_effects=True),
        cost_estimate=pl.CostEstimate(flops=10 ** 9, bytes_accessed=17 * 10 ** 6, transcendentals=0),
        name="project_second",
    )(prefix, pair, *shared, *weights)


BLOCK_KV = 512
WINDOW = 272


def attn_kernel(base_req, prefix_ref, valid_ref, qa_ref, ka_ref, va_ref, qb_ref, kb_ref, vb_ref, k_ref, v_ref, *refs):
    refs = refs[-23:]
    o_ref, ko_ref, vo_ref, kbuf, vbuf, obuf, qa, ka, va, qb, kb, vb, qbuf, fbuf, acc_ref, m_ref, l_ref, even_ref, odd_ref, k_sem, v_sem, out_sem, in_sem = refs
    n_req, heads = HALF_REQ, 3
    rows, dim = 4 * ROWS, HEAD
    slots = kbuf.shape[1]
    chip = lax.axis_index("tp") // 2
    ours = pl.ds(pl.multiple_of(chip * 2 * ROWS, 2 * ROWS), 2 * ROWS)
    theirs = pl.ds(pl.multiple_of((1 - chip) * 2 * ROWS, 2 * ROWS), 2 * ROWS)
    last = slots // BLOCK_KV - 1
    factor = (dim ** -0.5) * LOG2E

    def copies(r):
        at = base_req + r
        return (
            (pltpu.make_async_copy(k_ref.at[at], kbuf.at[r], k_sem.at[r]), pltpu.make_async_copy(v_ref.at[at], vbuf.at[r], v_sem.at[r])),
            (pltpu.make_async_copy(kbuf.at[r], ko_ref.at[at], out_sem.at[0, r]), pltpu.make_async_copy(vbuf.at[r], vo_ref.at[at], out_sem.at[1, r])),
            pltpu.make_async_copy(obuf.at[r], o_ref.at[r], out_sem.at[2, r]),
        )

    half = pl.ds(base_req, HALF_REQ)
    news = (
        pltpu.make_async_copy(ka_ref.at[half], ka, in_sem.at[0]),
        pltpu.make_async_copy(kb_ref, kb, in_sem.at[1]),
        pltpu.make_async_copy(va_ref.at[half], va, in_sem.at[2]),
        pltpu.make_async_copy(vb_ref, vb, in_sem.at[3]),
        pltpu.make_async_copy(qa_ref.at[half], qa, in_sem.at[4]),
        pltpu.make_async_copy(qb_ref, qb, in_sem.at[5]),
    )

    def merge(mine, far, buf, r, start, count):
        base = pl.multiple_of(jnp.minimum((start // 16) * 16, slots - WINDOW), 16)
        shift = start - base
        fbuf[ours, :] = mine.astype(jnp.float32)
        fbuf[theirs, :] = far.astype(jnp.float32)
        rolled = pltpu.roll(fbuf[...], shift, 0)
        idx = lax.broadcasted_iota(jnp.int32, rolled.shape, 0) - shift
        window = buf[r, pl.ds(base, WINDOW), :].astype(jnp.float32)
        merged = jnp.where((idx >= 0) & (idx < count), rolled, window)
        buf[r, pl.ds(base, WINDOW), :] = merged.astype(jnp.bfloat16)

    for copy in news:
        copy.start()

    @pl.loop(0, n_req)
    def _(r):
        for load in copies(r)[0]:
            load.start()

    fbuf[rows:, :] = jnp.zeros((WINDOW - rows, dim), jnp.float32)
    for copy in news:
        copy.wait()

    @pl.loop(0, n_req)
    def _(r):
        start = prefix_ref[base_req + r]
        count = valid_ref[base_req + r]
        loads, stores, give = copies(r)
        for load in loads:
            load.wait()
        merge(ka[r], kb[r], kbuf, r, start, count)
        merge(va[r], vb[r], vbuf, r, start, count)
        for store in stores:
            store.start()
        acc_ref[...] = jnp.zeros_like(acc_ref)
        l_ref[...] = jnp.zeros_like(l_ref)
        m_ref[...] = jnp.full_like(m_ref, -1.0e30)
        n_full = start // BLOCK_KV
        n_all = (start + count + BLOCK_KV - 1) // BLOCK_KV
        for h in range(heads):
            qbuf[h, ours, :] = qa[r, h]
            qbuf[h, theirs, :] = qb[r, h]
        wide = qbuf[...].reshape(heads * rows, dim).astype(jnp.float32) * factor
        high = wide.astype(jnp.bfloat16)
        low = (wide - high.astype(jnp.float32)).astype(jnp.bfloat16)
        queries = jnp.concatenate([high, low], axis=1)

        def scores(blk, dst):
            off = pl.multiple_of(jnp.minimum(blk, last) * BLOCK_KV, BLOCK_KV)
            keys = kbuf[r, pl.ds(off, BLOCK_KV), :]
            keys = jnp.concatenate([keys, keys], axis=1)
            s = lax.dot_general(queries, keys, (((1,), (1,)), ((), ())), preferred_element_type=jnp.float32)
            dst[...] = s

        def absorb(blk, src, masked):
            off = pl.multiple_of(blk * BLOCK_KV, BLOCK_KV)
            vals = vbuf[r, pl.ds(off, BLOCK_KV), :]
            s = src[...]
            if masked:
                row = lax.broadcasted_iota(jnp.int32, (rows, BLOCK_KV), 0)
                col = lax.broadcasted_iota(jnp.int32, (rows, BLOCK_KV), 1)
                visible = col + off <= start + jnp.minimum(row, count - 1)
                s = jnp.where(jnp.concatenate([visible] * heads, axis=0), s, -1.0e30)
            m_old = m_ref[...]
            best = jnp.max(s, axis=1, keepdims=True)
            m_new = jnp.maximum(m_old, best)
            alpha = jnp.exp2(m_old - m_new)
            p = jnp.exp2(s - m_new[:, :1])
            part = p[:, :128]
            for j in range(1, BLOCK_KV // 128):
                part = part + p[:, j * 128:(j + 1) * 128]
            l_ref[...] = l_ref[...] * alpha + part
            m_ref[...] = m_new
            acc_ref[...] = acc_ref[...] * alpha + jnp.dot(p.astype(jnp.bfloat16), vals, preferred_element_type=jnp.float32)

        def step(blk, masked):
            @pl.when(blk % 2 == 0)
            def _():
                scores(blk + 1, odd_ref)
                absorb(blk, even_ref, masked)

            @pl.when(blk % 2 == 1)
            def _():
                scores(blk + 1, even_ref)
                absorb(blk, odd_ref, masked)

        scores(0, even_ref)

        @pl.loop(0, n_full)
        def _(blk):
            step(blk, False)

        @pl.loop(n_full, n_all)
        def _(blk):
            step(blk, True)

        for h in range(heads):
            at = slice(h * rows, (h + 1) * rows)
            total = jnp.sum(l_ref[at], axis=1, keepdims=True)
            obuf[r, :, h * dim:(h + 1) * dim] = (acc_ref[at] / total).astype(jnp.bfloat16)
        give.start()

    @pl.loop(0, n_req)
    def _(r):
        _, stores, give = copies(r)
        for store in stores:
            store.wait()
        give.wait()


def attention(base_req, prefix, valid, mine, far, k_cache, v_cache, previous=()):
    part = (HALF_REQ, 2 * ROWS, HEAD)
    state = pltpu.VMEM((3 * 4 * ROWS, HEAD), jnp.float32)
    tile = pltpu.VMEM((3 * 4 * ROWS, BLOCK_KV), jnp.float32)
    slots = pltpu.VMEM((HALF_REQ,) + k_cache.shape[1:], jnp.bfloat16)
    q_part = pltpu.VMEM((HALF_REQ, 3, 2 * ROWS, HEAD), jnp.bfloat16)
    kv_part = pltpu.VMEM(part, jnp.bfloat16)
    return pl.pallas_call(
        functools.partial(attn_kernel, base_req),
        in_specs=[SMEM, SMEM] + [ANY] * (8 + len(previous)),
        out_specs=[ANY, ANY, ANY],
        scratch_shapes=[
            slots, slots, pltpu.VMEM((HALF_REQ, 4 * ROWS, 3 * HEAD), jnp.bfloat16),
            q_part, kv_part, kv_part, q_part, kv_part, kv_part,
            pltpu.VMEM((3, 4 * ROWS, HEAD), jnp.bfloat16),
            pltpu.VMEM((WINDOW, HEAD), jnp.float32),
            state, state, state, tile, tile,
            DMA((HALF_REQ,)), DMA((HALF_REQ,)), DMA((3, HALF_REQ)), DMA((6,)),
        ],
        out_shape=[
            jax.ShapeDtypeStruct((HALF_REQ, 4 * ROWS, 3 * HEAD), jnp.bfloat16),
            jax.ShapeDtypeStruct(k_cache.shape, jnp.bfloat16),
            jax.ShapeDtypeStruct(v_cache.shape, jnp.bfloat16),
        ],
        input_output_aliases={10 + i: 1 + i for i in range(len(previous))},
        cost_estimate=pl.CostEstimate(flops=10 ** 10, bytes_accessed=40 * 10 ** 6, transcendentals=7 * 10 ** 6),
        name="attention",
    )(prefix, valid, *mine, *far, k_cache, v_cache, *previous)


def mlp_kernel(o0_ref, o1_ref, x_ref, pair0_ref, pair1_ref, g_ref, wo_ref, near0_ref, across0_ref, near1_ref, wg_ref, wu_ref, wd_ref, out_ref,
               obuf, xin, wo, wg, wu, wd, hbuf, ubuf, psend, precv, pown, xsend, xrecv, x1buf,
               w_sem, wl_sem, in_sem, so, ro, lo, swy, rwy, swc, rwc, sh, rh, sp, rp, ss, rs):
    dp, peers = partners()
    me, core_peer, chip_peer, far_peer = peers
    other_dp = 1 - dp

    def cols(who):
        return pl.ds(pl.multiple_of(who * 384, 384), 384)

    def share(slot, g, s):
        block = peers[s] if slot == 0 else peers[s ^ 2]
        src = (o0_ref, o1_ref)[g].at[:, block]
        dst = obuf.at[slot, pl.ds(GROUP * g, GROUP), :, cols(me)]
        if s == 0:
            return pltpu.make_async_copy(src, dst, lo.at[slot, g])
        return send(src, dst, so.at[slot, g, s - 1], ro.at[slot, g, s - 1], (dp, peers[s]))

    def wo_rows(part, late):
        first = chip_peer * 384 + part * 192 + (WO_FIRST if late else 0)
        return wo.at[pl.ds(pl.multiple_of(first, 64), WO_REST if late else WO_FIRST)]

    own_rows = wo.at[pl.ds(pl.multiple_of(me * 384, 384), 384)]
    have = ((wo_ref, own_rows), (near0_ref, wo_rows(dp, False)), (across0_ref, wo_rows(other_dp, False)), (near1_ref, wo_rows(dp, True)))
    wo_local = tuple(pltpu.make_async_copy(src, dst, wl_sem.at[i]) for i, (src, dst) in enumerate(have))
    wo_dp = send(near1_ref, wo_rows(dp, True), swy, rwy, (other_dp, me))
    wo_core = tuple(send(src, dst, swc.at[i], rwc.at[i], (dp, core_peer)) for i, (src, dst) in enumerate(have))
    wo_last = send(wo_rows(other_dp, True), wo_rows(other_dp, True), swc.at[4], rwc.at[4], (dp, core_peer))
    weights = (
        pltpu.make_async_copy(wg_ref, wg.at[pl.ds(0, FFN)], w_sem.at[0]),
        pltpu.make_async_copy(wu_ref, wu.at[pl.ds(0, FFN)], w_sem.at[1]),
        pltpu.make_async_copy(wd_ref, wd.at[pl.ds(0, FFN)], w_sem.at[2]),
    )
    x_loads = (
        pltpu.make_async_copy(x_ref, xin.at[0], in_sem.at[0]),
        pltpu.make_async_copy(pair0_ref, xin.at[1, pl.ds(0, GROUP)], in_sem.at[1]),
        pltpu.make_async_copy(pair1_ref, xin.at[1, pl.ds(GROUP, GROUP)], in_sem.at[2]),
    )
    order = ((1, 0), (1, 1), (0, 0), (0, 1))

    greet([(dp, core_peer), (dp, chip_peer), (dp, far_peer), (other_dp, me)])
    wo_dp.start()
    for slot, g in order:
        for s in (2, 3, 1):
            share(slot, g, s).start()
    for copy in wo_core + wo_local:
        copy.start()
    for slot, g in order:
        share(slot, g, 0).start()
    for copy in x_loads + weights:
        copy.start()
    pad = jnp.zeros((FFN_PAD - FFN, WIDTH), jnp.bfloat16)
    for buf in (wg, wu, wd):
        buf[FFN:, :] = pad

    gain = g_ref[...].astype(jnp.float32).reshape(1, WIDTH)

    def give_h(k):
        return send(hbuf.at[k, 0], hbuf.at[k, 1], sh.at[k], rh.at[k], (dp, core_peer))

    def give_p(k):
        return send(psend.at[k], precv.at[k], sp.at[k], rp.at[k], (dp, core_peer))

    def give_s(g):
        return send(xsend.at[g], xrecv.at[g], ss.at[g], rs.at[g], (dp, chip_peer))

    def attn_out(k):
        slot, g = order[k]
        for s in (2, 3, 1):
            share(slot, g, s).wait_recv()
        share(slot, g, 0).wait()
        reqs = slice(GROUP * g, GROUP * (g + 1))
        heads = obuf[slot, reqs].reshape(GROUP * ROWS, WIDTH)
        attn = jnp.dot(heads, wo[...], preferred_element_type=jnp.float32).astype(jnp.bfloat16)
        base = xin[slot, reqs].reshape(GROUP * ROWS, WIDTH)
        mid = (base.astype(jnp.float32) + attn.astype(jnp.float32)).astype(jnp.bfloat16)
        if slot == 0:
            x1buf[g] = mid
        hbuf[k, 0] = rms_norm(mid.astype(jnp.float32), gain)
        give_h(k).start()

    def mlp(k):
        give_h(k).wait_recv()
        hidden = hbuf.at[k].reshape(2 * GROUP * ROWS, WIDTH)

        @pl.loop(0, FFN_PAD // FFN_TILE)
        def _(f):
            at = pl.ds(pl.multiple_of(f * FFN_TILE, FFN_TILE), FFN_TILE)
            nt = (((1,), (1,)), ((), ()))
            gate = lax.dot_general(hidden[...], wg[at, :], nt, preferred_element_type=jnp.float32)
            up = lax.dot_general(hidden[...], wu[at, :], nt, preferred_element_type=jnp.float32)
            ubuf[:, at] = (jax.nn.silu(gate) * up).astype(jnp.bfloat16)

        @pl.loop(0, WIDTH // OUT_TILE)
        def _(n):
            at = pl.ds(pl.multiple_of(n * OUT_TILE, OUT_TILE), OUT_TILE)
            down = jnp.dot(ubuf[...], wd[:, at], preferred_element_type=jnp.float32)
            pown[k, :, at] = down[:GROUP * ROWS]
            psend[k, :, at] = down[GROUP * ROWS:].astype(jnp.bfloat16)

        give_p(k).start()

    def combine(k):
        slot, g = order[k]
        give_p(k).wait_recv()
        total = pown[k] + precv[k].astype(jnp.float32)
        if slot == 1:
            xsend[g] = total.astype(jnp.bfloat16)
            give_s(g).start()
        else:
            give_s(g).wait_recv()
            down = (total + xrecv[g].astype(jnp.float32)).astype(jnp.bfloat16)
            out = (x1buf[g].astype(jnp.float32) + down.astype(jnp.float32)).astype(jnp.bfloat16)
            out_ref[GROUP * g:GROUP * (g + 1)] = out.reshape(GROUP, ROWS, WIDTH)

    wo_dp.wait_recv()
    wo_last.start()
    for copy in wo_local + x_loads:
        copy.wait()
    for copy in wo_core + (wo_last,):
        copy.wait_recv()
    attn_out(0)
    for copy in weights:
        copy.wait()
    mlp(0)
    attn_out(1)
    attn_out(2)
    combine(0)
    mlp(1)
    attn_out(3)
    combine(1)
    mlp(2)
    mlp(3)
    combine(2)
    combine(3)
    wo_dp.wait_send()
    for copy in wo_core + (wo_last,):
        copy.wait_send()
    for k, (slot, g) in enumerate(order):
        for s in (2, 3, 1):
            share(slot, g, s).wait_send()
        give_h(k).wait_send()
        give_p(k).wait_send()
    for g in range(2):
        give_s(g).wait_send()


def finish_layer(*operands):
    block = GROUP * ROWS
    return pl.pallas_call(
        mlp_kernel,
        in_specs=[ANY] * 5 + [VMEM] + [ANY] * 7,
        out_specs=VMEM,
        out_shape=jax.ShapeDtypeStruct((REQ, ROWS, WIDTH), jnp.bfloat16),
        scratch_shapes=[
            pltpu.VMEM((2, REQ, ROWS, WIDTH), jnp.bfloat16),
            pltpu.VMEM((2, REQ, ROWS, WIDTH), jnp.bfloat16),
            pltpu.VMEM((WIDTH, WIDTH), jnp.bfloat16),
            pltpu.VMEM((FFN_PAD, WIDTH), jnp.bfloat16),
            pltpu.VMEM((FFN_PAD, WIDTH), jnp.bfloat16),
            pltpu.VMEM((FFN_PAD, WIDTH), jnp.bfloat16),
            pltpu.VMEM((4, 2, block, WIDTH), jnp.bfloat16),
            pltpu.VMEM((2 * block, FFN_PAD), jnp.bfloat16),
            pltpu.VMEM((4, block, WIDTH), jnp.bfloat16),
            pltpu.VMEM((4, block, WIDTH), jnp.bfloat16),
            pltpu.VMEM((4, block, WIDTH), jnp.float32),
            pltpu.VMEM((2, block, WIDTH), jnp.bfloat16),
            pltpu.VMEM((2, block, WIDTH), jnp.bfloat16),
            pltpu.VMEM((2, block, WIDTH), jnp.bfloat16),
            DMA((3,)), DMA((4,)), DMA((3,)),
            DMA((2, 2, 3)), DMA((2, 2, 3)), DMA((2, 2)),
            DMA, DMA, DMA((5,)), DMA((5,)),
            DMA((4,)), DMA((4,)), DMA((4,)), DMA((4,)), DMA((2,)), DMA((2,)),
        ],
        compiler_params=pltpu.CompilerParams(collective_id=1, has_side_effects=True, vmem_limit_bytes=62 * 1024 * 1024),
        name="finish_layer",
    )(*operands)


def solution(mesh):
    row_spec = P("dp", "tp", None)
    cache_spec = P("dp", None, "tp", None)
    req_spec = P("dp")
    rep_spec = P(None)
    col_spec = P(None, "tp")
    bias_spec = P("tp")
    down_spec = P("tp", None)

    def layer(x_rows, k_cache, v_cache, prefix, valid, g_attn, w_q, b_q, w_k, b_k, w_v, b_v, w_o, g_mlp, w_gate, w_up, w_down):
        cache_shape = (REQ, k_cache.shape[1], HEAD)
        k_old, v_old = k_cache.reshape(cache_shape), v_cache.reshape(cache_shape)
        across_chips = [(0, 2), (1, 3), (2, 0), (3, 1)]
        shared = (g_attn, b_q, b_k, b_v) + rope_tables()
        weights = (w_q, w_k, w_v)
        *first, pair0, wo_first, wo_rest = project_first(prefix, x_rows, shared, weights, w_o)
        mine, far0 = first[:3], first[3:]
        x_late, far0[0] = lax.optimization_barrier((x_rows[HALF_REQ:], far0[0]))
        pair1 = lax.ppermute(x_late, "tp", across_chips)
        o0, k_out, v_out = attention(0, prefix, valid, mine, far0, k_old, v_old)
        wo_first, pair1, k_out = lax.optimization_barrier((wo_first, pair1, k_out))
        near0 = lax.ppermute(wo_first, "tp", across_chips)
        far1 = list(project_second(prefix, pair1, shared, weights))
        near0, wo_rest, far1[0] = lax.optimization_barrier((near0, wo_rest, far1[0]))
        across0 = lax.ppermute(near0, "dp", [(0, 1), (1, 0)])
        near1 = lax.ppermute(wo_rest, "tp", across_chips)
        o1, k_out, v_out = attention(HALF_REQ, prefix, valid, mine, far1, k_old, v_old, (k_out, v_out))
        blocks = (HALF_REQ, 4, ROWS, 3 * HEAD)
        x_out = finish_layer(o0.reshape(blocks), o1.reshape(blocks), x_rows, pair0, pair1, g_mlp, w_o, near0, across0, near1, w_gate.T, w_up.T, w_down)
        return x_out, k_out.reshape(k_cache.shape), v_out.reshape(v_cache.shape)

    in_specs = (row_spec, cache_spec, cache_spec, req_spec, req_spec, rep_spec, col_spec, bias_spec, col_spec, bias_spec, col_spec, bias_spec, down_spec, rep_spec, col_spec, col_spec, down_spec)
    return jax.shard_map(layer, mesh=mesh, in_specs=in_specs, out_specs=(row_spec, cache_spec, cache_spec), check_vma=False)
```

time: 152 us -> 132 us (0.87)
  Pallas kernels: 143 us -> 121 us
  starting transfers between devices: 0.05 us -> 3.02 us
  local copies, waits for them, and re-layouts: 6.75 us -> 4.31 us
    pallas_call x3 -> x5, Pallas kernels: 143 us -> 121 us  [the longest x1 64 us: finish_layer(): pl.pallas_call(mlp_kernel, in_specs=[ANY] * 5 + [VMEM] + [ANY] * 7, out_s...]
    ppermute x1 -> x4, starting transfers between devices: 0.05 us -> 3.02 us  [the longest x1 1.22 us: layer(): across0 = lax.ppermute(near0, 'dp', [(0, 1), (1, 0)])]
    broadcast_in_dim x3 -> x0, local copies, waits for them, and re-layouts: 2.45 us -> none  [the longest x1 1.29 us: project_rows(): g_attn[None]]
    unnamed x5 -> x13, local copies, waits for them, and re-layouts: 3.2 us -> 3.2 us
  transfers between devices with their start and end apart: 1 -> 4, of which waited for: 0 -> 1; matrix products, arithmetic and copies ran while one was open for 0% -> 0% of each run, Pallas kernels for 26% -> 27%
where the time goes in v1:
time: 132 us; the launch traced here: 131 us
  Pallas kernels  121 us (92%)
  local copies, waits for them, and re-layouts  4.31 us (3%)
  starting transfers between devices  3.02 us (2%)
    pallas_call x1, Pallas kernels, finish_layer(): pl.pallas_call(mlp_kernel, in_specs=[ANY] * 5 + [VMEM] + [ANY] * 7, out_s...  64 us
    pallas_call x2, Pallas kernels, attention(): pl.pallas_call(functools.partial(attn_kernel, base_req), in_specs=[SMEM,...  28.8 us
    pallas_call x1, Pallas kernels, project_first(): pl.pallas_call(first_kernel, in_specs=[SMEM, ANY] + [VMEM] * 7 + [ANY] *...  22.2 us
    pallas_call x1, Pallas kernels, project_second(): pl.pallas_call(second_kernel, in_specs=[SMEM, ANY] + [VMEM] * 7 + [ANY] *...  6.22 us
    unnamed x13, local copies, waits for them, and re-layouts  3.2 us
  transfers between devices with their start and end apart: 4, of which 1 were waited for; matrix products, arithmetic and copies ran while one was open for 0% of the time, Pallas kernels for 27%

profile of v1, /device:TPU:0, one launch (start us, length us, event | category | flops | bytes accessed | tf_op | source)
XLA Modules:
  0.0 130.5 jit_solution(6473347697083428365)
XLA Ops:
  0.6 1.1 slice.3
  1.7 22.2 %project_first.1 = (bf16[6,3,128,128]{3,2,1,0:T(8,128)(2,1)}, bf16[6,128,128]{2,1,0:T(8,128)(2,1)}, bf16[6,128,128]{2,1,0:T(8,128)(2,1)}, bf16[3,3,128,128]{3,2,...) custom-call(s32[6]{0:T(128)} %prefix_ref.7, ...), custom_call_target="tpu_custom_call" | custom-call | flops 2000000000 | bytes 60000000 | tf_op jit(solution)/shard_map/project_first/pallas_call | solution.py:211
  24.0 0.0 collective-permute-start
  24.0 0.0 copy-start.5
  24.0 0.0 copy-start.4
  24.0 14.9 %attention.2 = (bf16[3,256,384]{2,1,0:T(8,128)(2,1)}, bf16[6,3072,128]{2,1,0:T(8,128)(2,1)}, bf16[6,3072,128]{2,1,0:T(8,128)(2,1)}) custom-call(s32[6]{0:T(128)} %prefix_ref.7, s32[6]{0:T(128)} %valid_ref.3, bf16[6,3,128,128]{3,2,1,0:T(8,128)(2,1)} %get-tuple-element.29.qa_ref, bf16[6,128,128]{2,1,0:T(8,128)(2,1)} %get-tuple-element.30.ka_ref, ...), custom_call_target="tpu_custom_call" | custom-call | flops 10000000000 | bytes 40000000 | tf_op jit(solution)/shard_map/attention/pallas_call | solution.py:402
  38.9 1.2 collective-permute-done.pair_ref.pair1_ref
  40.1 0.0 copy-done.5
  40.1 0.8 collective-permute-start.1
  40.9 0.0 copy-done
  40.9 6.2 %project_second.1 = (bf16[3,3,128,128]{3,2,1,0:T(8,128)(2,1)}, bf16[3,128,128]{2,1,0:T(8,128)(2,1)}, bf16[3,128,128]{2,1,0:T(8,128)(2,1)}) custom-call(s32[6]{0:T(128)} %prefix_ref.7, bf16[3,64,1536]{2,1,0:T(8,128)(2,1)} %copy-done, bf16[1536]{0:T(1024)(128)(2,1)} %g_ref.4, bf16[384]{0:T(512)(128)(2,1)} %bq_ref.3, bf16[128]{0:T(256)(128)(2,1)} %bk_ref.3, ...), custom_call_target="tpu_custom_call" | custom-call | flops 1000000000 | bytes 17000000 | tf_op jit(solution)/shard_map/project_second/pallas_call | solution.py:235
  47.2 0.0 collective-permute-done.1.near0_ref
  47.2 0.0 copy-start.2
  47.2 1.2 collective-permute-start.2
  48.4 0.0 copy-done.4
  48.4 0.9 collective-permute-start.3
  49.3 14.0 %attention.3 = (bf16[3,256,384]{2,1,0:T(8,128)(2,1)}, bf16[6,3072,128]{2,1,0:T(8,128)(2,1)}, bf16[6,3072,128]{2,1,0:T(8,128)(2,1)}) custom-call(s32[6]{0:T(128)} %prefix_ref.7, s32[6]{0:T(128)} %valid_ref.3, bf16[6,3,128,128]{3,2,1,0:T(8,128)(2,1)} %get-tuple-element.29.qa_ref, ...), custom_call_target="tpu_custom_call", output_to_operand_aliasing={{1}: (10, {}), {2}: (11, {})} | custom-call | flops 10000000000 | bytes 40000000 | tf_op jit(solution)/shard_map/attention/pallas_call | solution.py:402
  63.3 0.0 collective-permute-done.2.across0_ref
  63.3 0.0 copy-start.3
  63.3 0.0 collective-permute-done.3.near1_ref
  63.4 0.6 copy-done.3
  64.0 0.2 copy-done.1
  64.2 64.0 %finish_layer.1 = bf16[6,64,1536]{2,1,0:T(8,128)(2,1)} custom-call(bf16[3,4,64,384]{3,2,1,0:T(8,128)(2,1)} %bitcast.14, bf16[3,4,64,384]{3,2,1,0:T(8,128)(2,1)} %bitcast.15, bf16[6,64,1536]{2,1,0:T(8,128)(2,1)} %x_ref.3, bf16[3,64,1536]{2,1,0:T(8,128)(2,1)} %get-tuple-element.50.pair0_ref, bf16[3,64,1536]{2,1,0:T(8,128)(2,1)} %copy-done, ...), custom_call_target="tpu_custom_call" | custom-call | tf_op jit(solution)/shard_map/finish_layer/pallas_call | solution.py:574
  128.2 2.4 %copy.30 = bf16[6,64,1536]{2,1,0:T(8,128)(2,1)} copy(bf16[6,64,1536]{2,1,0:T(8,128)(2,1)} %finish_layer.1) | data formatting | bytes 2359296
  (3 shorter events, 0.0 us)
Async XLA Ops:
  24.0 16.1 %collective-permute-start = (bf16[3,64,1536]{2,1,0:T(8,128)(2,1)S(1)}, bf16[3,64,1536]{2,1,0:T(8,128)(2,1)S(1)}, u32[]{:S(2)}, u32[]{:S(2)}) collective-permute-start(bf16[3,64,1536]{2,1,0:T(8,128)(2,1)S(1)} %slice.3), channel_id=1, source_target_pairs={{0,2},{1,3},{2,0},{3,1},{4,6},{5,7},{6,4},{7,5}} | collective-permute-start | bytes 1769480 | tf_op jit(solution)/shard_map/ppermute | solution.py:622
  24.0 16.1 %copy-start.5 = (bf16[64,1536]{1,0:T(8,128)(2,1)S(1)}, bf16[64,1536]{1,0:T(8,128)(2,1)}, u32[]{:S(2)}) copy-start(bf16[64,1536]{1,0:T(8,128)(2,1)} %get-tuple-element.40) | copy-start | bytes 589828
  24.0 24.4 %copy-start.4 = (bf16[128,1536]{1,0:T(8,128)(2,1)S(1)}, bf16[128,1536]{1,0:T(8,128)(2,1)}, u32[]{:S(2)}) copy-start(bf16[128,1536]{1,0:T(8,128)(2,1)} %get-tuple-element.52) | copy-start | bytes 1179652
  40.1 0.9 copy-start
  40.1 7.1 %collective-permute-start.1 = (bf16[64,1536]{1,0:T(8,128)(2,1)S(1)}, bf16[64,1536]{1,0:T(8,128)(2,1)S(1)}, u32[]{:S(2)}, u32[]{:S(2)}) collective-permute-start(bf16[64,1536]{1,0:T(8,128)(2,1)S(1)} %copy-done.5), channel_id=1, source_target_pairs={{0,2},{1,3},{2,0},{3,1},{4,6},{5,7},{6,4},{7,5}} | collective-permute-start | bytes 589832 | tf_op jit(solution)/shard_map/ppermute | solution.py:625
  47.2 16.1 %copy-start.2 = (bf16[64,1536]{1,0:T(8,128)(2,1)}, bf16[64,1536]{1,0:T(8,128)(2,1)S(1)}, u32[]{:S(2)}) copy-start(bf16[64,1536]{1,0:T(8,128)(2,1)S(1)} %collective-permute-done.1.near0_ref) | copy-start | bytes 589828
  47.2 16.1 %collective-permute-start.2 = (bf16[64,1536]{1,0:T(8,128)(2,1)S(1)}, bf16[64,1536]{1,0:T(8,128)(2,1)S(1)}, u32[]{:S(2)}, u32[]{:S(2)}) collective-permute-start(bf16[64,1536]{1,0:T(8,128)(2,1)S(1)} %collective-permute-done.1.near0_ref), channel_id=1, source_target_pairs={{0,4},{4,0},{1,5},{5,1},{2,6},{6,2},{3,7},{7,3}} | collective-permute-start | bytes 589832 | tf_op jit(solution)/shard_map/ppermute | solution.py:628
  48.4 14.9 %collective-permute-start.3 = (bf16[128,1536]{1,0:T(8,128)(2,1)S(1)}, bf16[128,1536]{1,0:T(8,128)(2,1)S(1)}, u32[]{:S(2)}, u32[]{:S(2)}) collective-permute-start(bf16[128,1536]{1,0:T(8,128)(2,1)S(1)} %copy-done.4), channel_id=1, source_target_pairs={{0,2},{1,3},{2,0},{3,1},{4,6},{5,7},{6,4},{7,5}} | collective-permute-start | bytes 1179656 | tf_op jit(solution)/shard_map/ppermute | solution.py:629
  63.3 0.7 copy-start.3
  63.3 0.8 copy-start.1

commit v2 on v1

v2 whole, which is shorter than its diff:
```python
import jax
import jax.numpy as jnp
import numpy as np
from jax import lax
from jax.experimental import pallas as pl
from jax.experimental.pallas import tpu as pltpu
from jax.sharding import PartitionSpec as P

ROPE_THETA = 1.0e6
NORM_EPS = 1.0e-6
LOG2E = 1.4426950408889634
MESH = pl.DeviceIdType.MESH
ANY = pl.BlockSpec(memory_space=pl.ANY)
VMEM = pl.BlockSpec(memory_space=pltpu.VMEM)
SMEM = pl.BlockSpec(memory_space=pltpu.SMEM)
DMA = pltpu.SemaphoreType.DMA
REQ = 6
ROWS = 64
WIDTH = 1536
HEAD = 128
FFN = 2240
FFN_PAD = 2304
FFN_TILE = 768
GROUP = 3
HALF_WIDTH = 768


def rms_norm(wide, gain):
    inv_rms = lax.rsqrt(jnp.mean(wide * wide, axis=-1, keepdims=True) + NORM_EPS)
    return (wide * inv_rms * gain).astype(jnp.bfloat16)


def partners():
    me = lax.axis_index("tp")
    chip, core = me // 2, me % 2
    return lax.axis_index("dp"), (me, chip * 2 + 1 - core, (1 - chip) * 2 + core, (1 - chip) * 2 + 1 - core)


def greet(devices):
    barrier = pltpu.get_barrier_semaphore()
    for device in devices:
        pl.semaphore_signal(barrier, inc=1, device_id=device, device_id_type=MESH)
    pl.semaphore_wait(barrier, len(devices))


def send(src, dst, send_sem, recv_sem, device):
    return pltpu.make_async_remote_copy(src_ref=src, dst_ref=dst, send_sem=send_sem, recv_sem=recv_sem, device_id=device, device_id_type=MESH)


def rope_tables():
    freq = ROPE_THETA ** (-(np.arange(HEAD // 2, dtype=np.float64) * 2.0) / HEAD)
    freq = np.concatenate([freq, freq])
    angles = np.arange(4 * ROWS, dtype=np.float64)[:, None] * freq
    return np.cos(angles).astype(np.float32), np.sin(angles).astype(np.float32), freq.astype(np.float32)[None]


def load_shared(refs, bufs, sem):
    gain, bq, bk, bv, cos, sin, freq, wq, wk, wv = refs
    small, wbuf = bufs[:7], bufs[7]
    pairs = list(zip((gain, bq, bk, bv, cos, sin, freq), small))
    pairs += [(wq, wbuf.at[:, pl.ds(0, 384)]), (wk, wbuf.at[:, pl.ds(384, 128)]), (wv, wbuf.at[:, pl.ds(512, 128)])]
    return [pltpu.make_async_copy(src, dst, sem.at[i]) for i, (src, dst) in enumerate(pairs)]


SHARED_SCRATCH = [
    pltpu.VMEM((WIDTH,), jnp.bfloat16), pltpu.VMEM((384,), jnp.bfloat16), pltpu.VMEM((128,), jnp.bfloat16), pltpu.VMEM((128,), jnp.bfloat16),
    pltpu.VMEM((4 * ROWS, HEAD), jnp.float32), pltpu.VMEM((4 * ROWS, HEAD), jnp.float32), pltpu.VMEM((1, HEAD), jnp.float32),
    pltpu.VMEM((WIDTH, 640), jnp.bfloat16), DMA((10,)),
]


def qkv_scratch(n_req):
    return [
        pltpu.VMEM((n_req, 3, 2 * ROWS, HEAD), jnp.bfloat16),
        pltpu.VMEM((n_req, 2 * ROWS, HEAD), jnp.bfloat16),
        pltpu.VMEM((n_req, 2 * ROWS, HEAD), jnp.bfloat16),
        DMA((3, n_req)),
    ]


def give_qkv(bufs, refs, sem, r):
    return [pltpu.make_async_copy(buf.at[r], ref.at[r], sem.at[i, r]) for i, (buf, ref) in enumerate(zip(bufs, refs))]


def project(x, position, chip, shared, outs, r):
    g_ref, *biases, cos_ref, sin_ref, freq_ref, wbuf = shared
    q_ref, k_ref, v_ref = outs
    rows = pl.ds(pl.multiple_of(chip * 2 * ROWS, 2 * ROWS), 2 * ROWS)
    normed = rms_norm(x.astype(jnp.float32), g_ref[...].astype(jnp.float32).reshape(1, WIDTH))
    total = jnp.dot(normed, wbuf[...], preferred_element_type=jnp.float32)
    angle = jnp.full((8, HEAD), position, jnp.int32).astype(jnp.float32) * freq_ref[...]
    cos_p, sin_p = jnp.cos(angle)[:1], jnp.sin(angle)[:1]
    cos_i, sin_i = cos_ref[rows, :], sin_ref[rows, :]
    cos_t = cos_p * cos_i - sin_p * sin_i
    sin_t = sin_p * cos_i + cos_p * sin_i
    lane = lax.broadcasted_iota(jnp.int32, sin_t.shape, 1)
    sin_t = jnp.where(lane < HEAD // 2, -sin_t, sin_t)
    bias = jnp.concatenate([b[...].astype(jnp.float32).reshape(1, b.shape[0]) for b in biases], axis=1)
    rounded = (total + bias).astype(jnp.bfloat16)
    for head in range(4):
        part = rounded[:, head * HEAD:(head + 1) * HEAD].astype(jnp.float32)
        turned = (part * cos_t + pltpu.roll(part, HEAD // 2, 1) * sin_t).astype(jnp.bfloat16)
        if head < 3:
            q_ref[r, head] = turned
        else:
            k_ref[r] = turned
    v_ref[r] = rounded[:, 4 * HEAD:]


def qkv_kernel(prefix_ref, x_ref, *refs):
    shared_refs, mine_refs, far_refs, pair_ref = refs[:10], refs[10:13], refs[13:16], refs[16]
    own, other = refs[17:19]
    shared, shared_sem = refs[19:27], refs[27]
    mine, mine_sem = refs[28:31], refs[31]
    far, far_sem = refs[32:35], refs[35]
    in_sem, out_sem, sx, rx, sc, rc, sf, rf = refs[36:]
    dp, (me, core_peer, chip_peer, _) = partners()
    chip, core = me // 2, me % 2
    load_x = pltpu.make_async_copy(x_ref, own.at[core], in_sem)
    load_x.start()
    loads = load_shared(shared_refs, shared, shared_sem)
    greet([(dp, core_peer), (dp, chip_peer)])
    load_x.wait()

    def to_chip(r):
        return send(own.at[core, r], other.at[core, r], sx.at[r], rx.at[r], (dp, chip_peer))

    def to_core(r):
        return send(own.at[core, r], own.at[core, r], sc.at[r], rc.at[r], (dp, core_peer))

    def forward(r):
        return send(other.at[core, r], other.at[core, r], sf.at[r], rf.at[r], (dp, core_peer))

    def keep(r):
        return pltpu.make_async_copy(other.at[core, r], pair_ref.at[r], out_sem.at[r])

    for r in range(REQ):
        to_chip(r).start()
    for r in range(REQ):
        to_core(r).start()
    for load in loads:
        load.start()
    for load in loads:
        load.wait()

    @pl.loop(0, REQ)
    def _(r):
        to_core(r).wait_recv()
        project(own[:, r].reshape(2 * ROWS, WIDTH), prefix_ref[r], chip, shared, mine, r)
        for copy in give_qkv(mine, mine_refs, mine_sem, r):
            copy.start()

    @pl.loop(0, REQ + 1)
    def _(r):
        @pl.when(r < REQ)
        def _():
            to_chip(r).wait_recv()
            forward(r).start()
            keep(r).start()

        @pl.when(r > 0)
        def _():
            forward(r - 1).wait_recv()
            project(other[:, r - 1].reshape(2 * ROWS, WIDTH), prefix_ref[r - 1], 1 - chip, shared, far, r - 1)
            for copy in give_qkv(far, far_refs, far_sem, r - 1):
                copy.start()

    @pl.loop(0, REQ)
    def _(r):
        to_core(r).wait_send()
        for copy in give_qkv(mine, mine_refs, mine_sem, r):
            copy.wait()
        to_chip(r).wait_send()
        forward(r).wait_send()
        keep(r).wait()
        for copy in give_qkv(far, far_refs, far_sem, r):
            copy.wait()


def qkv_shapes(n_req):
    return [
        jax.ShapeDtypeStruct((n_req, 3, 2 * ROWS, HEAD), jnp.bfloat16),
        jax.ShapeDtypeStruct((n_req, 2 * ROWS, HEAD), jnp.bfloat16),
        jax.ShapeDtypeStruct((n_req, 2 * ROWS, HEAD), jnp.bfloat16),
    ]


def project_rows(prefix, x_rows, shared):
    return pl.pallas_call(
        qkv_kernel,
        in_specs=[SMEM] + [ANY] * 11,
        out_specs=[ANY] * 7,
        out_shape=qkv_shapes(REQ) + qkv_shapes(REQ) + [jax.ShapeDtypeStruct((REQ, ROWS, WIDTH), jnp.bfloat16)],
        scratch_shapes=[
            pltpu.VMEM((2, REQ, ROWS, WIDTH), jnp.bfloat16),
            pltpu.VMEM((2, REQ, ROWS, WIDTH), jnp.bfloat16),
            *SHARED_SCRATCH, *qkv_scratch(REQ), *qkv_scratch(REQ),
            DMA, DMA((REQ,)), DMA((REQ,)), DMA((REQ,)), DMA((REQ,)), DMA((REQ,)), DMA((REQ,)), DMA((REQ,)),
        ],
        compiler_params=pltpu.CompilerParams(collective_id=0, has_side_effects=True),
        cost_estimate=pl.CostEstimate(flops=2 * 10 ** 9, bytes_accessed=60 * 10 ** 6, transcendentals=0),
        name="project_rows",
    )(prefix, x_rows, *shared)


BLOCK_KV = 512
WINDOW = 272


def attn_kernel(prefix_ref, valid_ref, qa_ref, ka_ref, va_ref, qb_ref, kb_ref, vb_ref, k_ref, v_ref, *refs):
    o_ref, ko_ref, vo_ref, kbuf, vbuf, obuf, qa, ka, va, qb, kb, vb, qbuf, fbuf, acc_ref, m_ref, l_ref, even_ref, odd_ref, k_sem, v_sem, out_sem, in_sem = refs
    n_req, heads = REQ, 3
    rows, dim = 4 * ROWS, HEAD
    slots = kbuf.shape[1]
    chip = lax.axis_index("tp") // 2
    ours = pl.ds(pl.multiple_of(chip * 2 * ROWS, 2 * ROWS), 2 * ROWS)
    theirs = pl.ds(pl.multiple_of((1 - chip) * 2 * ROWS, 2 * ROWS), 2 * ROWS)
    last = slots // BLOCK_KV - 1
    factor = (dim ** -0.5) * LOG2E

    def copies(r):
        return (
            (pltpu.make_async_copy(k_ref.at[r], kbuf.at[r], k_sem.at[r]), pltpu.make_async_copy(v_ref.at[r], vbuf.at[r], v_sem.at[r])),
            (pltpu.make_async_copy(kbuf.at[r], ko_ref.at[r], out_sem.at[0, r]), pltpu.make_async_copy(vbuf.at[r], vo_ref.at[r], out_sem.at[1, r])),
            pltpu.make_async_copy(obuf.at[r], o_ref.at[r], out_sem.at[2, r]),
        )

    news = (
        pltpu.make_async_copy(ka_ref, ka, in_sem.at[0]),
        pltpu.make_async_copy(kb_ref, kb, in_sem.at[1]),
        pltpu.make_async_copy(va_ref, va, in_sem.at[2]),
        pltpu.make_async_copy(vb_ref, vb, in_sem.at[3]),
        pltpu.make_async_copy(qa_ref, qa, in_sem.at[4]),
        pltpu.make_async_copy(qb_ref, qb, in_sem.at[5]),
    )

    def merge(mine, far, buf, r, start, count):
        base = pl.multiple_of(jnp.minimum((start // 16) * 16, slots - WINDOW), 16)
        shift = start - base
        fbuf[ours, :] = mine.astype(jnp.float32)
        fbuf[theirs, :] = far.astype(jnp.float32)
        rolled = pltpu.roll(fbuf[...], shift, 0)
        idx = lax.broadcasted_iota(jnp.int32, rolled.shape, 0) - shift
        window = buf[r, pl.ds(base, WINDOW), :].astype(jnp.float32)
        merged = jnp.where((idx >= 0) & (idx < count), rolled, window)
        buf[r, pl.ds(base, WINDOW), :] = merged.astype(jnp.bfloat16)

    for copy in news:
        copy.start()
    for load in copies(0)[0]:
        load.start()
    fbuf[rows:, :] = jnp.zeros((WINDOW - rows, dim), jnp.float32)
    for copy in news:
        copy.wait()

    @pl.loop(0, n_req)
    def _(r):
        start = prefix_ref[r]
        count = valid_ref[r]
        loads, stores, give = copies(r)
        for load in loads:
            load.wait()

        @pl.when(r + 1 < n_req)
        def _():
            for load in copies(r + 1)[0]:
                load.start()

        merge(ka[r], kb[r], kbuf, r, start, count)
        merge(va[r], vb[r], vbuf, r, start, count)
        for store in stores:
            store.start()
        acc_ref[...] = jnp.zeros_like(acc_ref)
        l_ref[...] = jnp.zeros_like(l_ref)
        m_ref[...] = jnp.full_like(m_ref, -1.0e30)
        n_full = start // BLOCK_KV
        n_all = (start + count + BLOCK_KV - 1) // BLOCK_KV
        for h in range(heads):
            qbuf[h, ours, :] = qa[r, h]
            qbuf[h, theirs, :] = qb[r, h]
        wide = qbuf[...].reshape(heads * rows, dim).astype(jnp.float32) * factor
        high = wide.astype(jnp.bfloat16)
        low = (wide - high.astype(jnp.float32)).astype(jnp.bfloat16)
        queries = jnp.concatenate([high, low], axis=1)

        def scores(blk, dst):
            off = pl.multiple_of(jnp.minimum(blk, last) * BLOCK_KV, BLOCK_KV)
            keys = kbuf[r, pl.ds(off, BLOCK_KV), :]
            keys = jnp.concatenate([keys, keys], axis=1)
            s = lax.dot_general(queries, keys, (((1,), (1,)), ((), ())), preferred_element_type=jnp.float32)
            dst[...] = s

        def absorb(blk, src, masked):
            off = pl.multiple_of(blk * BLOCK_KV, BLOCK_KV)
            vals = vbuf[r, pl.ds(off, BLOCK_KV), :]
            s = src[...]
            if masked:
                row = lax.broadcasted_iota(jnp.int32, (rows, BLOCK_KV), 0)
                col = lax.broadcasted_iota(jnp.int32, (rows, BLOCK_KV), 1)
                visible = col + off <= start + jnp.minimum(row, count - 1)
                s = jnp.where(jnp.concatenate([visible] * heads, axis=0), s, -1.0e30)
            m_old = m_ref[...]
            best = jnp.max(s, axis=1, keepdims=True)
            m_new = jnp.maximum(m_old, best)
            alpha = jnp.exp2(m_old - m_new)
            p = jnp.exp2(s - m_new[:, :1])
            part = p[:, :128]
            for j in range(1, BLOCK_KV // 128):
                part = part + p[:, j * 128:(j + 1) * 128]
            l_ref[...] = l_ref[...] * alpha + part
            m_ref[...] = m_new
            acc_ref[...] = acc_ref[...] * alpha + jnp.dot(p.astype(jnp.bfloat16), vals, preferred_element_type=jnp.float32)

        def step(blk, masked):
            @pl.when(blk % 2 == 0)
            def _():
                scores(blk + 1, odd_ref)
                absorb(blk, even_ref, masked)

            @pl.when(blk % 2 == 1)
            def _():
                scores(blk + 1, even_ref)
                absorb(blk, odd_ref, masked)

        scores(0, even_ref)

        @pl.loop(0, n_full)
        def _(blk):
            step(blk, False)

        @pl.loop(n_full, n_all)
        def _(blk):
            step(blk, True)

        for h in range(heads):
            at = slice(h * rows, (h + 1) * rows)
            total = jnp.sum(l_ref[at], axis=1, keepdims=True)
            obuf[r, :, h * dim:(h + 1) * dim] = (acc_ref[at] / total).astype(jnp.bfloat16)
        give.start()

    @pl.loop(0, n_req)
    def _(r):
        _, stores, give = copies(r)
        for store in stores:
            store.wait()
        give.wait()


def attention(prefix, valid, mine, far, k_cache, v_cache):
    part = (REQ, 2 * ROWS, HEAD)
    state = pltpu.VMEM((3 * 4 * ROWS, HEAD), jnp.float32)
    tile = pltpu.VMEM((3 * 4 * ROWS, BLOCK_KV), jnp.float32)
    slots = pltpu.VMEM((REQ,) + k_cache.shape[1:], jnp.bfloat16)
    q_part = pltpu.VMEM((REQ, 3, 2 * ROWS, HEAD), jnp.bfloat16)
    kv_part = pltpu.VMEM(part, jnp.bfloat16)
    return pl.pallas_call(
        attn_kernel,
        in_specs=[SMEM, SMEM] + [ANY] * 8,
        out_specs=[ANY, ANY, ANY],
        scratch_shapes=[
            slots, slots, pltpu.VMEM((REQ, 4 * ROWS, 3 * HEAD), jnp.bfloat16),
            q_part, kv_part, kv_part, q_part, kv_part, kv_part,
            pltpu.VMEM((3, 4 * ROWS, HEAD), jnp.bfloat16),
            pltpu.VMEM((WINDOW, HEAD), jnp.float32),
            state, state, state, tile, tile,
            DMA((REQ,)), DMA((REQ,)), DMA((3, REQ)), DMA((6,)),
        ],
        out_shape=[
            jax.ShapeDtypeStruct((REQ, 4 * ROWS, 3 * HEAD), jnp.bfloat16),
            jax.ShapeDtypeStruct(k_cache.shape, jnp.bfloat16),
            jax.ShapeDtypeStruct(v_cache.shape, jnp.bfloat16),
        ],
        cost_estimate=pl.CostEstimate(flops=10 ** 10, bytes_accessed=40 * 10 ** 6, transcendentals=7 * 10 ** 6),
        name="attention",
    )(prefix, valid, *mine, *far, k_cache, v_cache)


def mlp_kernel(o_ref, x_ref, pair_ref, g_ref, wo_ref, far_ref, wg_ref, wu_ref, wd_ref, out_ref,
               osrc, obuf, xin, wo, wg, wu, wd, hbuf, ubuf, psend, precv, pown, xsend, xrecv, x1buf, outbuf,
               w_sem, wl_sem, in_sem, o_sem, so, ro, lo, swc, rwc, sh, rh, sp, rp, ss, rs):
    dp, peers = partners()
    me, core_peer, chip_peer, far_peer = peers

    def cols(who):
        return pl.ds(pl.multiple_of(who * 384, 384), 384)

    def share(slot, g, s):
        block = peers[s] if slot == 0 else peers[s ^ 2]
        src = (o_ref if s == 0 else osrc).at[pl.ds(GROUP * g, GROUP), block]
        dst = obuf.at[slot, pl.ds(GROUP * g, GROUP), :, cols(me)]
        if s == 0:
            return pltpu.make_async_copy(src, dst, lo.at[slot, g])
        return send(src, dst, so.at[slot, g, s - 1], ro.at[slot, g, s - 1], (dp, peers[s]))

    have = tuple((src, wo.at[pl.ds(pl.multiple_of(who * 384, 384), 384)]) for src, who in ((wo_ref, me), (far_ref, chip_peer)))
    wo_local = tuple(pltpu.make_async_copy(src, dst, wl_sem.at[i]) for i, (src, dst) in enumerate(have))
    wo_core = tuple(send(src, dst, swc.at[i], rwc.at[i], (dp, core_peer)) for i, (src, dst) in enumerate(have))
    weights = (
        pltpu.make_async_copy(wg_ref, wg.at[pl.ds(0, FFN)], w_sem.at[0]),
        pltpu.make_async_copy(wu_ref, wu.at[pl.ds(0, FFN)], w_sem.at[1]),
        pltpu.make_async_copy(wd_ref, wd.at[pl.ds(0, FFN)], w_sem.at[2]),
    )
    x_loads = (
        pltpu.make_async_copy(x_ref, xin.at[0], in_sem.at[0]),
        pltpu.make_async_copy(pair_ref, xin.at[1], in_sem.at[1]),
    )
    order = ((1, 0), (1, 1), (0, 0), (0, 1))

    load_o = pltpu.make_async_copy(o_ref, osrc, in_sem.at[2])
    load_o.start()
    for copy in wo_local + x_loads:
        copy.start()
    greet([(dp, core_peer), (dp, chip_peer), (dp, far_peer)])
    load_o.wait()
    for slot, g in order:
        for s in (2, 3, 1):
            share(slot, g, s).start()
    for copy in wo_core:
        copy.start()
    for slot, g in order:
        share(slot, g, 0).start()
    pad = jnp.zeros((FFN_PAD - FFN, WIDTH), jnp.bfloat16)
    for buf in (wg, wu, wd):
        buf[FFN:, :] = pad

    gain = g_ref[...].astype(jnp.float32).reshape(1, WIDTH)

    def give_h(k):
        return send(hbuf.at[k, 0], hbuf.at[k, 1], sh.at[k], rh.at[k], (dp, core_peer))

    def part(n):
        return pl.ds(pl.multiple_of(n * HALF_WIDTH, HALF_WIDTH), HALF_WIDTH)

    def give_p(k, n):
        return send(psend.at[k, :, part(n)], precv.at[k, :, part(n)], sp.at[k, n], rp.at[k, n], (dp, core_peer))

    def give_s(g, n):
        return send(xsend.at[g, :, part(n)], xrecv.at[g, :, part(n)], ss.at[g, n], rs.at[g, n], (dp, chip_peer))

    def give_out(g, n):
        reqs = pl.ds(GROUP * g, GROUP)
        return pltpu.make_async_copy(outbuf.at[reqs, :, part(n)], out_ref.at[reqs, :, part(n)], o_sem.at[g, n])

    def attn_out(k):
        slot, g = order[k]
        for s in (2, 3, 1):
            share(slot, g, s).wait_recv()
        share(slot, g, 0).wait()
        reqs = slice(GROUP * g, GROUP * (g + 1))
        heads = obuf[slot, reqs].reshape(GROUP * ROWS, WIDTH)
        attn = jnp.dot(heads, wo[...], preferred_element_type=jnp.float32).astype(jnp.bfloat16)
        base = xin[slot, reqs].reshape(GROUP * ROWS, WIDTH)
        mid = (base.astype(jnp.float32) + attn.astype(jnp.float32)).astype(jnp.bfloat16)
        if slot == 0:
            x1buf[g] = mid
        hbuf[k, 0] = rms_norm(mid.astype(jnp.float32), gain)
        give_h(k).start()

    def mlp(k):
        give_h(k).wait_recv()
        if k == 0:
            weights[0].wait()
            weights[1].wait()
        hidden = hbuf.at[k].reshape(2 * GROUP * ROWS, WIDTH)

        @pl.loop(0, FFN_PAD // FFN_TILE)
        def _(f):
            at = pl.ds(pl.multiple_of(f * FFN_TILE, FFN_TILE), FFN_TILE)
            nt = (((1,), (1,)), ((), ()))
            gate = lax.dot_general(hidden[...], wg[at, :], nt, preferred_element_type=jnp.float32)
            up = lax.dot_general(hidden[...], wu[at, :], nt, preferred_element_type=jnp.float32)
            ubuf[:, at] = (jax.nn.silu(gate) * up).astype(jnp.bfloat16)

        if k == 0:
            weights[2].wait()

        @pl.loop(0, 2)
        def _(n):
            down = jnp.dot(ubuf[...], wd[:, part(n)], preferred_element_type=jnp.float32)
            pown[k, :, part(n)] = down[:GROUP * ROWS]
            psend[k, :, part(n)] = down[GROUP * ROWS:].astype(jnp.bfloat16)
            give_p(k, n).start()

    def combine(k):
        slot, g = order[k]

        @pl.loop(0, 2)
        def _(n):
            give_p(k, n).wait_recv()
            total = pown[k, :, part(n)] + precv[k, :, part(n)].astype(jnp.float32)
            if slot == 1:
                xsend[g, :, part(n)] = total.astype(jnp.bfloat16)
                give_s(g, n).start()
            else:
                give_s(g, n).wait_recv()
                down = (total + xrecv[g, :, part(n)].astype(jnp.float32)).astype(jnp.bfloat16)
                out = (x1buf[g, :, part(n)].astype(jnp.float32) + down.astype(jnp.float32)).astype(jnp.bfloat16)
                outbuf[GROUP * g:GROUP * (g + 1), :, part(n)] = out.reshape(GROUP, ROWS, HALF_WIDTH)
                give_out(g, n).start()

    for copy in wo_local + x_loads:
        copy.wait()
    for copy in weights:
        copy.start()
    for copy in wo_core:
        copy.wait_recv()
    attn_out(0)
    mlp(0)
    attn_out(1)
    attn_out(2)
    combine(0)
    mlp(1)
    attn_out(3)
    combine(1)
    mlp(2)
    combine(2)
    mlp(3)
    combine(3)
    for copy in wo_core:
        copy.wait_send()
    for k, (slot, g) in enumerate(order):
        for s in (2, 3, 1):
            share(slot, g, s).wait_send()
        give_h(k).wait_send()
        for n in range(2):
            give_p(k, n).wait_send()
    for g in range(2):
        for n in range(2):
            give_s(g, n).wait_send()
            give_out(g, n).wait()


def finish_layer(*operands):
    block = GROUP * ROWS
    return pl.pallas_call(
        mlp_kernel,
        in_specs=[ANY] * 3 + [VMEM] + [ANY] * 5,
        out_specs=ANY,
        out_shape=jax.ShapeDtypeStruct((REQ, ROWS, WIDTH), jnp.bfloat16),
        scratch_shapes=[
            pltpu.VMEM((REQ, 4, ROWS, 3 * HEAD), jnp.bfloat16),
            pltpu.VMEM((2, REQ, ROWS, WIDTH), jnp.bfloat16),
            pltpu.VMEM((2, REQ, ROWS, WIDTH), jnp.bfloat16),
            pltpu.VMEM((WIDTH, WIDTH), jnp.bfloat16),
            pltpu.VMEM((FFN_PAD, WIDTH), jnp.bfloat16),
            pltpu.VMEM((FFN_PAD, WIDTH), jnp.bfloat16),
            pltpu.VMEM((FFN_PAD, WIDTH), jnp.bfloat16),
            pltpu.VMEM((4, 2, block, WIDTH), jnp.bfloat16),
            pltpu.VMEM((2 * block, FFN_PAD), jnp.bfloat16),
            pltpu.VMEM((4, block, WIDTH), jnp.bfloat16),
            pltpu.VMEM((4, block, WIDTH), jnp.bfloat16),
            pltpu.VMEM((4, block, WIDTH), jnp.float32),
            pltpu.VMEM((2, block, WIDTH), jnp.bfloat16),
            pltpu.VMEM((2, block, WIDTH), jnp.bfloat16),
            pltpu.VMEM((2, block, WIDTH), jnp.bfloat16),
            pltpu.VMEM((REQ, ROWS, WIDTH), jnp.bfloat16),
            DMA((3,)), DMA((2,)), DMA((3,)), DMA((2, 2)),
            DMA((2, 2, 3)), DMA((2, 2, 3)), DMA((2, 2)),
            DMA((2,)), DMA((2,)),
            DMA((4,)), DMA((4,)), DMA((4, 2)), DMA((4, 2)), DMA((2, 2)), DMA((2, 2)),
        ],
        compiler_params=pltpu.CompilerParams(collective_id=1, has_side_effects=True, vmem_limit_bytes=62 * 1024 * 1024),
        name="finish_layer",
    )(*operands)


def solution(mesh):
    row_spec = P("dp", "tp", None)
    cache_spec = P("dp", None, "tp", None)
    req_spec = P("dp")
    rep_spec = P(None)
    col_spec = P(None, "tp")
    bias_spec = P("tp")
    down_spec = P("tp", None)

    def layer(x_rows, k_cache, v_cache, prefix, valid, g_attn, w_q, b_q, w_k, b_k, w_v, b_v, w_o, g_mlp, w_gate, w_up, w_down):
        cache_shape = (REQ, k_cache.shape[1], HEAD)
        k_old, v_old = k_cache.reshape(cache_shape), v_cache.reshape(cache_shape)
        across_chips = [(0, 2), (1, 3), (2, 0), (3, 1)]
        shared = (g_attn, b_q, b_k, b_v) + rope_tables() + (w_q, w_k, w_v)
        *qkv, x_pair = project_rows(prefix, x_rows, shared)
        mine, far = qkv[:3], qkv[3:]
        w_own, far[0] = lax.optimization_barrier((w_o, far[0]))
        w_far = lax.ppermute(w_own, "tp", across_chips)
        o, k_out, v_out = attention(prefix, valid, mine, far, k_old, v_old)
        x_out = finish_layer(o.reshape(REQ, 4, ROWS, 3 * HEAD), x_rows, x_pair, g_mlp, w_o, w_far, w_gate.T, w_up.T, w_down)
        return x_out, k_out.reshape(k_cache.shape), v_out.reshape(v_cache.shape)

    in_specs = (row_spec, cache_spec, cache_spec, req_spec, req_spec, rep_spec, col_spec, bias_spec, col_spec, bias_spec, col_spec, bias_spec, down_spec, rep_spec, col_spec, col_spec, down_spec)
    return jax.shard_map(layer, mesh=mesh, in_specs=in_specs, out_specs=(row_spec, cache_spec, cache_spec), check_vma=False)
```

time: 132 us -> 128 us (0.970)
  Pallas kernels: 121 us -> 113 us
  waiting for transfers between devices: 1.19 us -> 8.38 us
  starting transfers between devices: 3.02 us -> 0.5 us
    pallas_call x5 -> x3, Pallas kernels: 121 us -> 113 us  [the longest x1 58.9 us: finish_layer(): pl.pallas_call(mlp_kernel, in_specs=[ANY] * 3 + [VMEM] + [ANY] * 5, out_s...]
    ppermute x4 -> x1, waiting for transfers between devices: 1.19 us -> 8.38 us  [layer(): w_far = lax.ppermute(w_own, 'tp', across_chips)]
    ppermute x4 -> x1, starting transfers between devices: 3.02 us -> 0.5 us  [layer(): w_far = lax.ppermute(w_own, 'tp', across_chips)]
    unnamed x13 -> x5, local copies, waits for them, and re-layouts: 3.2 us -> 3.42 us
  transfers between devices with their start and end apart: 4 -> 1, of which waited for: 1 -> 1; matrix products, arithmetic and copies ran while one was open for 0% -> 0% of each run, Pallas kernels for 27% -> 16%
where the time goes in v2:
time: 128 us; the launch traced here: 126 us
  Pallas kernels  113 us (88%)
  waiting for transfers between devices  8.38 us (7%)
  local copies, waits for them, and re-layouts  3.42 us (3%)
    pallas_call x1, Pallas kernels, finish_layer(): pl.pallas_call(mlp_kernel, in_specs=[ANY] * 3 + [VMEM] + [ANY] * 5, out_s...  58.9 us
    pallas_call x1, Pallas kernels, project_rows(): pl.pallas_call(qkv_kernel, in_specs=[SMEM] + [ANY] * 11, out_specs=[ANY]...  34 us
    pallas_call x1, Pallas kernels, attention(): pl.pallas_call(attn_kernel, in_specs=[SMEM, SMEM] + [ANY] * 8, out_specs=...  19.9 us
    ppermute x1, waiting for transfers between devices, layer(): w_far = lax.ppermute(w_own, 'tp', across_chips)  8.38 us
    unnamed x5, local copies, waits for them, and re-layouts  3.42 us
  transfers between devices with their start and end apart: 1, of which 1 were waited for; matrix products, arithmetic and copies ran while one was open for 0% of the time, Pallas kernels for 16%

profile of v2, /device:TPU:0, one launch (start us, length us, event | category | flops | bytes accessed | tf_op | source)
XLA Modules:
  0.0 125.8 jit_solution(17557138382686453329)
XLA Ops:
  0.6 0.0 copy-start
  0.6 34.0 %project_rows.1 = (bf16[6,3,128,128]{3,2,1,0:T(8,128)(2,1)}, bf16[6,128,128]{2,1,0:T(8,128)(2,1)}, bf16[6,128,128]{2,1,0:T(8,128)(2,1)}, bf16[6,3,128,128]{3,2,1...) custom-call(s32[6]{0:T(128)} %prefix_ref.3, ...), custom_call_target="tpu_custom_call" | custom-call | flops 2000000000 | bytes 60000000 | tf_op jit(solution)/shard_map/project_rows/pallas_call | solution.py:189
  34.7 0.0 copy-done
  34.7 0.5 collective-permute-start
  35.2 19.9 %attention.1 = (bf16[6,256,384]{2,1,0:T(8,128)(2,1)}, bf16[6,3072,128]{2,1,0:T(8,128)(2,1)}, bf16[6,3072,128]{2,1,0:T(8,128)(2,1)}) custom-call(s32[6]{0:T(128)} %prefix_ref.3, s32[6]{0:T(128)} %valid_ref.1, bf16[6,3,128,128]{3,2,1,0:T(8,128)(2,1)} %get-tuple-element.15.qa_ref, bf16[6,128,128]{2,1,0:T(8,128)(2,1)} %get-tuple-element.16.ka_ref, ...), custom_call_target="tpu_custom_call" | custom-call | flops 10000000000 | bytes 40000000 | tf_op jit(solution)/shard_map/attention/pallas_call | solution.py:356
  55.1 8.4 %collective-permute-done.far_ref = bf16[384,1536]{1,0:T(8,128)(2,1)S(1)} collective-permute-done((bf16[384,1536]{1,0:T(8,128)(2,1)S(1)}, bf16[384,1536]{1,0:T(8,128)(2,1)S(1)}, u32[]{:S(2)}, u32[]{:S(2)}) %collective-permute-start) | collective-permute-done | bytes 1179680 | tf_op jit(solution)/shard_map/ppermute | solution.py:584
  63.4 0.0 copy-start.1
  63.4 1.0 copy-done.1
  64.5 58.9 %finish_layer.1 = bf16[6,64,1536]{2,1,0:T(8,128)(2,1)} custom-call(bf16[6,4,64,384]{3,2,1,0:T(8,128)(2,1)} %bitcast.13, bf16[6,64,1536]{2,1,0:T(8,128)(2,1)} %x_ref.3, bf16[6,64,1536]{2,1,0:T(8,128)(2,1)} %get-tuple-element.23.pair_ref, bf16[1536]{0:T(1024)(128)(2,1)} %g_ref.1, bf16[384,1536]{1,0:T(8,128)(2,1)} %wo_ref.1, bf16[384,1536]{1,0:T(8,128)(2,1)} %copy-done.1, ...), custom_call_target="tpu_custom_call" | custom-call | tf_op jit(solution)/shard_map/finish_layer/pallas_call | solution.py:535
  123.4 2.4 %copy.26 = bf16[6,64,1536]{2,1,0:T(8,128)(2,1)} copy(bf16[6,64,1536]{2,1,0:T(8,128)(2,1)} %finish_layer.1) | data formatting | bytes 2359296
Async XLA Ops:
  0.6 34.1 %copy-start = (bf16[384,1536]{1,0:T(8,128)(2,1)S(1)}, bf16[384,1536]{1,0:T(8,128)(2,1)}, u32[]{:S(2)}) copy-start(bf16[384,1536]{1,0:T(8,128)(2,1)} %wo_ref.1) | copy-start | bytes 3538948
  34.7 28.7 %collective-permute-start = (bf16[384,1536]{1,0:T(8,128)(2,1)S(1)}, bf16[384,1536]{1,0:T(8,128)(2,1)S(1)}, u32[]{:S(2)}, u32[]{:S(2)}) collective-permute-start(bf16[384,1536]{1,0:T(8,128)(2,1)S(1)} %copy-done), channel_id=1, source_target_pairs={{0,2},{1,3},{2,0},{3,1},{4,6},{5,7},{6,4},{7,5}} | collective-permute-start | bytes 3538952 | tf_op jit(solution)/shard_map/ppermute | solution.py:584
  63.4 1.0 copy-start.1

commit v3 on v2

--- a/solution.py
+++ b/solution.py
@@ -21,7 +21,12 @@
 FFN = 2240
 FFN_PAD = 2304
 FFN_TILE = 768
-GROUP = 3
+WO_EARLY = 32
+STEPS = ((1, 0, 2), (1, 2, 2), (1, 4, 2), (0, 0, 3), (0, 3, 3))
+STEP_ROWS = [ROWS * sum(n for _, _, n in STEPS[:k]) for k in range(len(STEPS))]
+RS_NEED = {3: (0, 1), 4: (2,)}
+ALL_ROWS = 2 * REQ * ROWS
+MAX_ROWS = 2 * ROWS * max(n for _, _, n in STEPS)
 HALF_WIDTH = 768
 
 
@@ -108,12 +113,12 @@
 
 
 def qkv_kernel(prefix_ref, x_ref, *refs):
-    shared_refs, mine_refs, far_refs, pair_ref = refs[:10], refs[10:13], refs[13:16], refs[16]
-    own, other = refs[17:19]
-    shared, shared_sem = refs[19:27], refs[27]
-    mine, mine_sem = refs[28:31], refs[31]
-    far, far_sem = refs[32:35], refs[35]
-    in_sem, out_sem, sx, rx, sc, rc, sf, rf = refs[36:]
+    shared_refs, wo_ref, mine_refs, far_refs, pair_ref, early_ref = refs[:10], refs[10], refs[11:14], refs[14:17], refs[17], refs[18]
+    late_ref, own, other, late = refs[19:23]
+    shared, shared_sem = refs[23:31], refs[31]
+    mine, mine_sem = refs[32:35], refs[35]
+    far, far_sem = refs[36:39], refs[39]
+    in_sem, out_sem, sx, rx, sc, rc, sf, rf, se, re, late_sem = refs[40:]
     dp, (me, core_peer, chip_peer, _) = partners()
     chip, core = me // 2, me % 2
     load_x = pltpu.make_async_copy(x_ref, own.at[core], in_sem)
@@ -134,14 +139,21 @@
     def keep(r):
         return pltpu.make_async_copy(other.at[core, r], pair_ref.at[r], out_sem.at[r])
 
+    early = send(wo_ref.at[pl.ds(0, WO_EARLY)], early_ref, se, re, (dp, chip_peer))
     for r in range(REQ):
         to_chip(r).start()
+    early.start()
     for r in range(REQ):
         to_core(r).start()
+    take_late = pltpu.make_async_copy(wo_ref.at[pl.ds(WO_EARLY, 384 - WO_EARLY)], late, late_sem.at[0])
+    give_late = pltpu.make_async_copy(late, late_ref, late_sem.at[1])
     for load in loads:
         load.start()
+    take_late.start()
     for load in loads:
         load.wait()
+    take_late.wait()
+    give_late.start()
 
     @pl.loop(0, REQ)
     def _(r):
@@ -164,6 +176,9 @@
             project(other[:, r - 1].reshape(2 * ROWS, WIDTH), prefix_ref[r - 1], 1 - chip, shared, far, r - 1)
             for copy in give_qkv(far, far_refs, far_sem, r - 1):
                 copy.start()
+
+    early.wait()
+    give_late.wait()
 
     @pl.loop(0, REQ)
     def _(r):
@@ -185,22 +200,27 @@
     ]
 
 
-def project_rows(prefix, x_rows, shared):
+def project_rows(prefix, x_rows, shared, w_o):
     return pl.pallas_call(
         qkv_kernel,
-        in_specs=[SMEM] + [ANY] * 11,
-        out_specs=[ANY] * 7,
-        out_shape=qkv_shapes(REQ) + qkv_shapes(REQ) + [jax.ShapeDtypeStruct((REQ, ROWS, WIDTH), jnp.bfloat16)],
+        in_specs=[SMEM] + [ANY] * 12,
+        out_specs=[ANY] * 9,
+        out_shape=qkv_shapes(REQ) + qkv_shapes(REQ) + [
+            jax.ShapeDtypeStruct((REQ, ROWS, WIDTH), jnp.bfloat16),
+            jax.ShapeDtypeStruct((WO_EARLY, WIDTH), jnp.bfloat16),
+            jax.ShapeDtypeStruct((384 - WO_EARLY, WIDTH), jnp.bfloat16),
+        ],
         scratch_shapes=[
             pltpu.VMEM((2, REQ, ROWS, WIDTH), jnp.bfloat16),
             pltpu.VMEM((2, REQ, ROWS, WIDTH), jnp.bfloat16),
+            pltpu.VMEM((384 - WO_EARLY, WIDTH), jnp.bfloat16),
             *SHARED_SCRATCH, *qkv_scratch(REQ), *qkv_scratch(REQ),
-            DMA, DMA((REQ,)), DMA((REQ,)), DMA((REQ,)), DMA((REQ,)), DMA((REQ,)), DMA((REQ,)), DMA((REQ,)),
+            DMA, DMA((REQ,)), DMA((REQ,)), DMA((REQ,)), DMA((REQ,)), DMA((REQ,)), DMA((REQ,)), DMA((REQ,)), DMA, DMA, DMA((2,)),
         ],
         compiler_params=pltpu.CompilerParams(collective_id=0, has_side_effects=True),
         cost_estimate=pl.CostEstimate(flops=2 * 10 ** 9, bytes_accessed=60 * 10 ** 6, transcendentals=0),
         name="project_rows",
-    )(prefix, x_rows, *shared)
+    )(prefix, x_rows, *shared, w_o)
 
 
 BLOCK_KV = 512
@@ -247,8 +267,9 @@
 
     for copy in news:
         copy.start()
-    for load in copies(0)[0]:
-        load.start()
+    for r in range(2):
+        for load in copies(r)[0]:
+            load.start()
     fbuf[rows:, :] = jnp.zeros((WINDOW - rows, dim), jnp.float32)
     for copy in news:
         copy.wait()
@@ -261,9 +282,9 @@
         for load in loads:
             load.wait()
 
-        @pl.when(r + 1 < n_req)
+        @pl.when(r + 2 < n_req)
         def _():
-            for load in copies(r + 1)[0]:
+            for load in copies(r + 2)[0]:
                 load.start()
 
         merge(ka[r], kb[r], kbuf, r, start, count)
@@ -371,11 +392,12 @@
             jax.ShapeDtypeStruct(v_cache.shape, jnp.bfloat16),
         ],
         cost_estimate=pl.CostEstimate(flops=10 ** 10, bytes_accessed=40 * 10 ** 6, transcendentals=7 * 10 ** 6),
+        compiler_params=pltpu.CompilerParams(vmem_limit_bytes=67_043_328),
         name="attention",
     )(prefix, valid, *mine, *far, k_cache, v_cache)
 
 
-def mlp_kernel(o_ref, x_ref, pair_ref, g_ref, wo_ref, far_ref, wg_ref, wu_ref, wd_ref, out_ref,
+def mlp_kernel(o_ref, x_ref, pair_ref, g_ref, wo_ref, early_ref, far_ref, wg_ref, wu_ref, wd_ref, out_ref,
                osrc, obuf, xin, wo, wg, wu, wd, hbuf, ubuf, psend, precv, pown, xsend, xrecv, x1buf, outbuf,
                w_sem, wl_sem, in_sem, o_sem, so, ro, lo, swc, rwc, sh, rh, sp, rp, ss, rs):
     dp, peers = partners()
@@ -384,15 +406,23 @@
     def cols(who):
         return pl.ds(pl.multiple_of(who * 384, 384), 384)
 
-    def share(slot, g, s):
+    def share(k, s):
+        slot, first, n = STEPS[k]
         block = peers[s] if slot == 0 else peers[s ^ 2]
-        src = (o_ref if s == 0 else osrc).at[pl.ds(GROUP * g, GROUP), block]
-        dst = obuf.at[slot, pl.ds(GROUP * g, GROUP), :, cols(me)]
+        src = (o_ref if s == 0 else osrc).at[pl.ds(first, n), block]
+        dst = obuf.at[slot, pl.ds(first, n), :, cols(me)]
         if s == 0:
-            return pltpu.make_async_copy(src, dst, lo.at[slot, g])
-        return send(src, dst, so.at[slot, g, s - 1], ro.at[slot, g, s - 1], (dp, peers[s]))
-
-    have = tuple((src, wo.at[pl.ds(pl.multiple_of(who * 384, 384), 384)]) for src, who in ((wo_ref, me), (far_ref, chip_peer)))
+            return pltpu.make_async_copy(src, dst, lo.at[k])
+        return send(src, dst, so.at[k, s - 1], ro.at[k, s - 1], (dp, peers[s]))
+
+    def wo_rows(who, first, count):
+        return wo.at[pl.ds(pl.multiple_of(who * 384 + first, 32), count)]
+
+    have = (
+        (wo_ref, wo_rows(me, 0, 384)),
+        (early_ref, wo_rows(chip_peer, 0, WO_EARLY)),
+        (far_ref, wo_rows(chip_peer, WO_EARLY, 384 - WO_EARLY)),
+    )
     wo_local = tuple(pltpu.make_async_copy(src, dst, wl_sem.at[i]) for i, (src, dst) in enumerate(have))
     wo_core = tuple(send(src, dst, swc.at[i], rwc.at[i], (dp, core_peer)) for i, (src, dst) in enumerate(have))
     weights = (
@@ -404,7 +434,7 @@
         pltpu.make_async_copy(x_ref, xin.at[0], in_sem.at[0]),
         pltpu.make_async_copy(pair_ref, xin.at[1], in_sem.at[1]),
     )
-    order = ((1, 0), (1, 1), (0, 0), (0, 1))
+    steps = range(len(STEPS))
 
     load_o = pltpu.make_async_copy(o_ref, osrc, in_sem.at[2])
     load_o.start()
@@ -412,91 +442,105 @@
         copy.start()
     greet([(dp, core_peer), (dp, chip_peer), (dp, far_peer)])
     load_o.wait()
-    for slot, g in order:
+    for k in steps:
         for s in (2, 3, 1):
-            share(slot, g, s).start()
+            share(k, s).start()
     for copy in wo_core:
         copy.start()
-    for slot, g in order:
-        share(slot, g, 0).start()
+    for k in steps:
+        share(k, 0).start()
     pad = jnp.zeros((FFN_PAD - FFN, WIDTH), jnp.bfloat16)
     for buf in (wg, wu, wd):
         buf[FFN:, :] = pad
 
     gain = g_ref[...].astype(jnp.float32).reshape(1, WIDTH)
 
+    def half_rows(k):
+        return STEPS[k][2] * ROWS
+
     def give_h(k):
-        return send(hbuf.at[k, 0], hbuf.at[k, 1], sh.at[k], rh.at[k], (dp, core_peer))
+        mine = hbuf.at[pl.ds(2 * STEP_ROWS[k], half_rows(k))]
+        theirs = hbuf.at[pl.ds(2 * STEP_ROWS[k] + half_rows(k), half_rows(k))]
+        return send(mine, theirs, sh.at[k], rh.at[k], (dp, core_peer))
 
     def part(n):
         return pl.ds(pl.multiple_of(n * HALF_WIDTH, HALF_WIDTH), HALF_WIDTH)
 
     def give_p(k, n):
-        return send(psend.at[k, :, part(n)], precv.at[k, :, part(n)], sp.at[k, n], rp.at[k, n], (dp, core_peer))
-
-    def give_s(g, n):
-        return send(xsend.at[g, :, part(n)], xrecv.at[g, :, part(n)], ss.at[g, n], rs.at[g, n], (dp, chip_peer))
-
-    def give_out(g, n):
-        reqs = pl.ds(GROUP * g, GROUP)
-        return pltpu.make_async_copy(outbuf.at[reqs, :, part(n)], out_ref.at[reqs, :, part(n)], o_sem.at[g, n])
+        at = pl.ds(STEP_ROWS[k], half_rows(k))
+        return send(psend.at[at, part(n)], precv.at[at, part(n)], sp.at[k, n], rp.at[k, n], (dp, core_peer))
+
+    def give_s(k, n):
+        at = pl.ds(STEPS[k][1] * ROWS, half_rows(k))
+        return send(xsend.at[at, part(n)], xrecv.at[at, part(n)], ss.at[k, n], rs.at[k, n], (dp, chip_peer))
+
+    def give_out(k, n):
+        reqs = pl.ds(STEPS[k][1], STEPS[k][2])
+        return pltpu.make_async_copy(outbuf.at[reqs, :, part(n)], out_ref.at[reqs, :, part(n)], o_sem.at[k, n])
 
     def attn_out(k):
-        slot, g = order[k]
+        slot, first, n = STEPS[k]
+        m = half_rows(k)
         for s in (2, 3, 1):
-            share(slot, g, s).wait_recv()
-        share(slot, g, 0).wait()
-        reqs = slice(GROUP * g, GROUP * (g + 1))
-        heads = obuf[slot, reqs].reshape(GROUP * ROWS, WIDTH)
+            share(k, s).wait_recv()
+        share(k, 0).wait()
+        heads = obuf[slot, first:first + n].reshape(m, WIDTH)
         attn = jnp.dot(heads, wo[...], preferred_element_type=jnp.float32).astype(jnp.bfloat16)
-        base = xin[slot, reqs].reshape(GROUP * ROWS, WIDTH)
+        base = xin[slot, first:first + n].reshape(m, WIDTH)
         mid = (base.astype(jnp.float32) + attn.astype(jnp.float32)).astype(jnp.bfloat16)
         if slot == 0:
-            x1buf[g] = mid
-        hbuf[k, 0] = rms_norm(mid.astype(jnp.float32), gain)
+            x1buf[first * ROWS:first * ROWS + m] = mid
+        hbuf[2 * STEP_ROWS[k]:2 * STEP_ROWS[k] + m] = rms_norm(mid.astype(jnp.float32), gain)
         give_h(k).start()
 
-    def mlp(k):
+    def widen(k):
         give_h(k).wait_recv()
         if k == 0:
             weights[0].wait()
             weights[1].wait()
-        hidden = hbuf.at[k].reshape(2 * GROUP * ROWS, WIDTH)
+        rows = pl.ds(2 * STEP_ROWS[k], 2 * half_rows(k))
 
         @pl.loop(0, FFN_PAD // FFN_TILE)
         def _(f):
             at = pl.ds(pl.multiple_of(f * FFN_TILE, FFN_TILE), FFN_TILE)
             nt = (((1,), (1,)), ((), ()))
-            gate = lax.dot_general(hidden[...], wg[at, :], nt, preferred_element_type=jnp.float32)
-            up = lax.dot_general(hidden[...], wu[at, :], nt, preferred_element_type=jnp.float32)
-            ubuf[:, at] = (jax.nn.silu(gate) * up).astype(jnp.bfloat16)
-
+            gate = lax.dot_general(hbuf[rows, :], wg[at, :], nt, preferred_element_type=jnp.float32)
+            up = lax.dot_general(hbuf[rows, :], wu[at, :], nt, preferred_element_type=jnp.float32)
+            ubuf[:2 * half_rows(k), at] = (jax.nn.silu(gate) * up).astype(jnp.bfloat16)
+
+    def narrow(k):
+        m = half_rows(k)
+        at = slice(STEP_ROWS[k], STEP_ROWS[k] + m)
         if k == 0:
             weights[2].wait()
 
         @pl.loop(0, 2)
         def _(n):
-            down = jnp.dot(ubuf[...], wd[:, part(n)], preferred_element_type=jnp.float32)
-            pown[k, :, part(n)] = down[:GROUP * ROWS]
-            psend[k, :, part(n)] = down[GROUP * ROWS:].astype(jnp.bfloat16)
+            down = jnp.dot(ubuf[:2 * m, :], wd[:, part(n)], preferred_element_type=jnp.float32)
+            pown[at, part(n)] = down[:m]
+            psend[at, part(n)] = down[m:].astype(jnp.bfloat16)
             give_p(k, n).start()
 
     def combine(k):
-        slot, g = order[k]
+        slot, first, count = STEPS[k]
+        m = half_rows(k)
+        at = slice(STEP_ROWS[k], STEP_ROWS[k] + m)
+        mine = slice(first * ROWS, first * ROWS + m)
 
         @pl.loop(0, 2)
         def _(n):
             give_p(k, n).wait_recv()
-            total = pown[k, :, part(n)] + precv[k, :, part(n)].astype(jnp.float32)
+            total = pown[at, part(n)] + precv[at, part(n)].astype(jnp.float32)
             if slot == 1:
-                xsend[g, :, part(n)] = total.astype(jnp.bfloat16)
-                give_s(g, n).start()
+                xsend[mine, part(n)] = total.astype(jnp.bfloat16)
+                give_s(k, n).start()
             else:
-                give_s(g, n).wait_recv()
-                down = (total + xrecv[g, :, part(n)].astype(jnp.float32)).astype(jnp.bfloat16)
-                out = (x1buf[g, :, part(n)].astype(jnp.float32) + down.astype(jnp.float32)).astype(jnp.bfloat16)
-                outbuf[GROUP * g:GROUP * (g + 1), :, part(n)] = out.reshape(GROUP, ROWS, HALF_WIDTH)
-                give_out(g, n).start()
+                for j in RS_NEED[k]:
+                    give_s(j, n).wait_recv()
+                down = (total + xrecv[mine, part(n)].astype(jnp.float32)).astype(jnp.bfloat16)
+                out = (x1buf[mine, part(n)].astype(jnp.float32) + down.astype(jnp.float32)).astype(jnp.bfloat16)
+                outbuf[first:first + count, :, part(n)] = out.reshape(count, ROWS, HALF_WIDTH)
+                give_out(k, n).start()
 
     for copy in wo_local + x_loads:
         copy.wait()
@@ -505,36 +549,32 @@
     for copy in wo_core:
         copy.wait_recv()
     attn_out(0)
-    mlp(0)
-    attn_out(1)
-    attn_out(2)
-    combine(0)
-    mlp(1)
-    attn_out(3)
-    combine(1)
-    mlp(2)
-    combine(2)
-    mlp(3)
-    combine(3)
+    for k in steps:
+        widen(k)
+        if k + 1 < len(STEPS):
+            attn_out(k + 1)
+        if k > 0:
+            combine(k - 1)
+        narrow(k)
+    combine(len(STEPS) - 1)
     for copy in wo_core:
         copy.wait_send()
-    for k, (slot, g) in enumerate(order):
+    for k in steps:
         for s in (2, 3, 1):
-            share(slot, g, s).wait_send()
+            share(k, s).wait_send()
         give_h(k).wait_send()
         for n in range(2):
             give_p(k, n).wait_send()
-    for g in range(2):
-        for n in range(2):
-            give_s(g, n).wait_send()
-            give_out(g, n).wait()
+            if STEPS[k][0] == 1:
+                give_s(k, n).wait_send()
+            else:
+                give_out(k, n).wait()
 
 
 def finish_layer(*operands):
-    block = GROUP * ROWS
     return pl.pallas_call(
         mlp_kernel,
-        in_specs=[ANY] * 3 + [VMEM] + [ANY] * 5,
+        in_specs=[ANY] * 3 + [VMEM] + [ANY] * 6,
         out_specs=ANY,
         out_shape=jax.ShapeDtypeStruct((REQ, ROWS, WIDTH), jnp.bfloat16),
         scratch_shapes=[
@@ -545,19 +585,19 @@
             pltpu.VMEM((FFN_PAD, WIDTH), jnp.bfloat16),
             pltpu.VMEM((FFN_PAD, WIDTH), jnp.bfloat16),
             pltpu.VMEM((FFN_PAD, WIDTH), jnp.bfloat16),
-            pltpu.VMEM((4, 2, block, WIDTH), jnp.bfloat16),
-            pltpu.VMEM((2 * block, FFN_PAD), jnp.bfloat16),
-            pltpu.VMEM((4, block, WIDTH), jnp.bfloat16),
-            pltpu.VMEM((4, block, WIDTH), jnp.bfloat16),
-            pltpu.VMEM((4, block, WIDTH), jnp.float32),
-            pltpu.VMEM((2, block, WIDTH), jnp.bfloat16),
-            pltpu.VMEM((2, block, WIDTH), jnp.bfloat16),
-            pltpu.VMEM((2, block, WIDTH), jnp.bfloat16),
+            pltpu.VMEM((2 * ALL_ROWS, WIDTH), jnp.bfloat16),
+            pltpu.VMEM((MAX_ROWS, FFN_PAD), jnp.bfloat16),
+            pltpu.VMEM((ALL_ROWS, WIDTH), jnp.bfloat16),
+            pltpu.VMEM((ALL_ROWS, WIDTH), jnp.bfloat16),
+            pltpu.VMEM((ALL_ROWS, WIDTH), jnp.float32),
+            pltpu.VMEM((REQ * ROWS, WIDTH), jnp.bfloat16),
+            pltpu.VMEM((REQ * ROWS, WIDTH), jnp.bfloat16),
+            pltpu.VMEM((REQ * ROWS, WIDTH), jnp.bfloat16),
             pltpu.VMEM((REQ, ROWS, WIDTH), jnp.bfloat16),
-            DMA((3,)), DMA((2,)), DMA((3,)), DMA((2, 2)),
-            DMA((2, 2, 3)), DMA((2, 2, 3)), DMA((2, 2)),
-            DMA((2,)), DMA((2,)),
-            DMA((4,)), DMA((4,)), DMA((4, 2)), DMA((4, 2)), DMA((2, 2)), DMA((2, 2)),
+            DMA((3,)), DMA((3,)), DMA((3,)), DMA((5, 2)),
+            DMA((5, 3)), DMA((5, 3)), DMA((5,)),
+            DMA((3,)), DMA((3,)),
+            DMA((5,)), DMA((5,)), DMA((5, 2)), DMA((5, 2)), DMA((3, 2)), DMA((3, 2)),
         ],
         compiler_params=pltpu.CompilerParams(collective_id=1, has_side_effects=True, vmem_limit_bytes=62 * 1024 * 1024),
         name="finish_layer",
@@ -578,12 +618,12 @@
         k_old, v_old = k_cache.reshape(cache_shape), v_cache.reshape(cache_shape)
         across_chips = [(0, 2), (1, 3), (2, 0), (3, 1)]
         shared = (g_attn, b_q, b_k, b_v) + rope_tables() + (w_q, w_k, w_v)
-        *qkv, x_pair = project_rows(prefix, x_rows, shared)
+        *qkv, x_pair, w_early, w_late = project_rows(prefix, x_rows, shared, w_o)
         mine, far = qkv[:3], qkv[3:]
-        w_own, far[0] = lax.optimization_barrier((w_o, far[0]))
+        w_own, far[0] = lax.optimization_barrier((w_late, far[0]))
         w_far = lax.ppermute(w_own, "tp", across_chips)
         o, k_out, v_out = attention(prefix, valid, mine, far, k_old, v_old)
-        x_out = finish_layer(o.reshape(REQ, 4, ROWS, 3 * HEAD), x_rows, x_pair, g_mlp, w_o, w_far, w_gate.T, w_up.T, w_down)
+        x_out = finish_layer(o.reshape(REQ, 4, ROWS, 3 * HEAD), x_rows, x_pair, g_mlp, w_o, w_early, w_far, w_gate.T, w_up.T, w_down)
         return x_out, k_out.reshape(k_cache.shape), v_out.reshape(v_cache.shape)
 
     in_specs = (row_spec, cache_spec, cache_spec, req_spec, req_spec, rep_spec, col_spec, bias_spec, col_spec, bias_spec, col_spec, bias_spec, down_spec, rep_spec, col_spec, col_spec, down_spec)

time: 128 us -> 123 us (0.961); the launches traced: 126 us -> 122 us
  waiting for transfers between devices: 8.38 us -> 0.01 us
  Pallas kernels: 113 us -> 119 us
    ppermute x1, waiting for transfers between devices: 8.38 us -> 0.01 us  [layer(): w_far = lax.ppermute(w_own, 'tp', across_chips)]
    pallas_call x1, Pallas kernels: 19.9 us -> 26.3 us  [attention(): pl.pallas_call(attn_kernel, in_specs=[SMEM, SMEM] + [ANY] * 8, out_specs=...]
    unnamed x5 -> x1, local copies, waits for them, and re-layouts: 3.42 us -> 2.39 us
  transfers between devices with their start and end apart: 1 -> 1, of which waited for: 1 -> 0; matrix products, arithmetic and copies ran while one was open for 0% -> 0% of each run, Pallas kernels for 16% -> 21%
where the time goes in v3:
time: 123 us; the launch traced here: 122 us
  Pallas kernels  119 us (97%)
  local copies, waits for them, and re-layouts  2.39 us (2%)
    pallas_call x1, Pallas kernels, finish_layer(): pl.pallas_call(mlp_kernel, in_specs=[ANY] * 3 + [VMEM] + [ANY] * 6, out_s...  57.5 us
    pallas_call x1, Pallas kernels, project_rows(): pl.pallas_call(qkv_kernel, in_specs=[SMEM] + [ANY] * 12, out_specs=[ANY]...  34.8 us
    pallas_call x1, Pallas kernels, attention(): pl.pallas_call(attn_kernel, in_specs=[SMEM, SMEM] + [ANY] * 8, out_specs=...  26.3 us
  transfers between devices with their start and end apart: 1, of which 0 were waited for; matrix products, arithmetic and copies ran while one was open for 0% of the time, Pallas kernels for 21%

profile of v3, /device:TPU:0, one launch (start us, length us, event | category | flops | bytes accessed | tf_op | source)
XLA Modules:
  0.0 122.3 jit_solution(12246717192113556294)
XLA Ops:
  0.6 34.8 %project_rows.1 = (bf16[6,3,128,128]{3,2,1,0:T(8,128)(2,1)}, bf16[6,128,128]{2,1,0:T(8,128)(2,1)}, bf16[6,128,128]{2,1,0:T(8,128)(2,1)}, bf16[6,3,128,128]{3,2,1...) custom-call(s32[6]{0:T(128)} %prefix_ref.3, ...), custom_call_target="tpu_custom_call" | custom-call | flops 2000000000 | bytes 60000000 | tf_op jit(solution)/shard_map/project_rows/pallas_call | solution.py:204
  35.4 0.7 collective-permute-start
  36.1 26.3 %attention.1 = (bf16[6,256,384]{2,1,0:T(8,128)(2,1)}, bf16[6,3072,128]{2,1,0:T(8,128)(2,1)}, bf16[6,3072,128]{2,1,0:T(8,128)(2,1)}) custom-call(s32[6]{0:T(128)} %prefix_ref.3, s32[6]{0:T(128)} %valid_ref.1, bf16[6,3,128,128]{3,2,1,0:T(8,128)(2,1)} %get-tuple-element.17.qa_ref, bf16[6,128,128]{2,1,0:T(8,128)(2,1)} %get-tuple-element.18.ka_ref, ...), custom_call_target="tpu_custom_call" | custom-call | flops 10000000000 | bytes 40000000 | tf_op jit(solution)/shard_map/attention/pallas_call | solution.py:377
  62.4 0.0 collective-permute-done.far_ref
  62.4 57.5 %finish_layer.1 = bf16[6,64,1536]{2,1,0:T(8,128)(2,1)} custom-call(bf16[6,4,64,384]{3,2,1,0:T(8,128)(2,1)} %bitcast.13, bf16[6,64,1536]{2,1,0:T(8,128)(2,1)} %x_ref.3, bf16[6,64,1536]{2,1,0:T(8,128)(2,1)} %get-tuple-element.26.pair_ref, bf16[1536]{0:T(1024)(128)(2,1)} %g_ref.1, bf16[384,1536]{1,0:T(8,128)(2,1)} %wo_ref.1, ...), custom_call_target="tpu_custom_call" | custom-call | tf_op jit(solution)/shard_map/finish_layer/pallas_call | solution.py:575
  120.0 2.4 %copy.26 = bf16[6,64,1536]{2,1,0:T(8,128)(2,1)} copy(bf16[6,64,1536]{2,1,0:T(8,128)(2,1)} %finish_layer.1) | data formatting | bytes 2359296
Async XLA Ops:
  35.4 27.0 %collective-permute-start = (bf16[352,1536]{1,0:T(8,128)(2,1)}, bf16[352,1536]{1,0:T(8,128)(2,1)}, u32[]{:S(2)}, u32[]{:S(2)}) collective-permute-start(bf16[352,1536]{1,0:T(8,128)(2,1)} %get-tuple-element.28), channel_id=1, source_target_pairs={{0,2},{1,3},{2,0},{3,1},{4,6},{5,7},{6,4},{7,5}} | collective-permute-start | bytes 3244040 | tf_op jit(solution)/shard_map/ppermute | solution.py:624

commit v4 on v3

--- a/solution.py
+++ b/solution.py
@@ -349,9 +349,17 @@
         def _(blk):
             step(blk, False)
 
-        @pl.loop(n_full, n_all)
+        @pl.loop(n_full, n_all - 1)
         def _(blk):
             step(blk, True)
+
+        @pl.when(n_all % 2 == 1)
+        def _():
+            absorb(n_all - 1, even_ref, True)
+
+        @pl.when(n_all % 2 == 0)
+        def _():
+            absorb(n_all - 1, odd_ref, True)
 
         for h in range(heads):
             at = slice(h * rows, (h + 1) * rows)

time: 123 us -> 125 us (1.016)
    pallas_call x1, Pallas kernels: 26.3 us -> 27.5 us  [attention(): pl.pallas_call(attn_kernel, in_specs=[SMEM, SMEM] + [ANY] * 8, out_specs=...]
  transfers between devices with their start and end apart: 1 -> 1, of which waited for: 0 -> 0; matrix products, arithmetic and copies ran while one was open for 0% -> 0% of each run, Pallas kernels for 21% -> 22%
where the time goes in v4:
time: 125 us; the launch traced here: 124 us
  Pallas kernels  120 us (96%)
  local copies, waits for them, and re-layouts  2.39 us (2%)
    pallas_call x1, Pallas kernels, finish_layer(): pl.pallas_call(mlp_kernel, in_specs=[ANY] * 3 + [VMEM] + [ANY] * 6, out_s...  57.5 us
    pallas_call x1, Pallas kernels, project_rows(): pl.pallas_call(qkv_kernel, in_specs=[SMEM] + [ANY] * 12, out_specs=[ANY]...  34.8 us
    pallas_call x1, Pallas kernels, attention(): pl.pallas_call(attn_kernel, in_specs=[SMEM, SMEM] + [ANY] * 8, out_specs=...  27.5 us
  transfers between devices with their start and end apart: 1, of which 0 were waited for; matrix products, arithmetic and copies ran while one was open for 0% of the time, Pallas kernels for 22%

profile of v4, /device:TPU:0, one launch (start us, length us, event | category | flops | bytes accessed | tf_op | source)
XLA Modules:
  0.0 123.6 jit_solution(10383479954238140936)
XLA Ops:
  0.6 34.8 %project_rows.1 = (bf16[6,3,128,128]{3,2,1,0:T(8,128)(2,1)}, bf16[6,128,128]{2,1,0:T(8,128)(2,1)}, bf16[6,128,128]{2,1,0:T(8,128)(2,1)}, bf16[6,3,128,128]{3,2,1...) custom-call(s32[6]{0:T(128)} %prefix_ref.3, ...), custom_call_target="tpu_custom_call" | custom-call | flops 2000000000 | bytes 60000000 | tf_op jit(solution)/shard_map/project_rows/pallas_call | solution.py:204
  35.4 0.7 collective-permute-start
  36.1 27.5 %attention.1 = (bf16[6,256,384]{2,1,0:T(8,128)(2,1)}, bf16[6,3072,128]{2,1,0:T(8,128)(2,1)}, bf16[6,3072,128]{2,1,0:T(8,128)(2,1)}) custom-call(s32[6]{0:T(128)} %prefix_ref.3, s32[6]{0:T(128)} %valid_ref.1, bf16[6,3,128,128]{3,2,1,0:T(8,128)(2,1)} %get-tuple-element.17.qa_ref, bf16[6,128,128]{2,1,0:T(8,128)(2,1)} %get-tuple-element.18.ka_ref, ...), custom_call_target="tpu_custom_call" | custom-call | flops 10000000000 | bytes 40000000 | tf_op jit(solution)/shard_map/attention/pallas_call | solution.py:385
  63.7 0.0 collective-permute-done.far_ref
  63.7 57.5 %finish_layer.1 = bf16[6,64,1536]{2,1,0:T(8,128)(2,1)} custom-call(bf16[6,4,64,384]{3,2,1,0:T(8,128)(2,1)} %bitcast.13, bf16[6,64,1536]{2,1,0:T(8,128)(2,1)} %x_ref.3, bf16[6,64,1536]{2,1,0:T(8,128)(2,1)} %get-tuple-element.26.pair_ref, bf16[1536]{0:T(1024)(128)(2,1)} %g_ref.1, bf16[384,1536]{1,0:T(8,128)(2,1)} %wo_ref.1, ...), custom_call_target="tpu_custom_call" | custom-call | tf_op jit(solution)/shard_map/finish_layer/pallas_call | solution.py:583
  121.3 2.4 %copy.26 = bf16[6,64,1536]{2,1,0:T(8,128)(2,1)} copy(bf16[6,64,1536]{2,1,0:T(8,128)(2,1)} %finish_layer.1) | data formatting | bytes 2359296
Async XLA Ops:
  35.4 28.3 %collective-permute-start = (bf16[352,1536]{1,0:T(8,128)(2,1)}, bf16[352,1536]{1,0:T(8,128)(2,1)}, u32[]{:S(2)}, u32[]{:S(2)}) collective-permute-start(bf16[352,1536]{1,0:T(8,128)(2,1)} %get-tuple-element.28), channel_id=1, source_target_pairs={{0,2},{1,3},{2,0},{3,1},{4,6},{5,7},{6,4},{7,5}} | collective-permute-start | bytes 3244040 | tf_op jit(solution)/shard_map/ppermute | solution.py:632
